TPU v7x, 512 devices: a whole 4x8x8 slice. The times are simulated.
512 devices in a mesh: vocab: 64 (over y, x, core), grp: 8 (over z).
Axes of the slice: x: 4, y: 8, z: 8, core: 2. Of those that a mesh axis runs over, the one named last changes fastest.
Arguments:
- hidden: bfloat16 [2048, 4096], P('grp'), may hold values from -240 to 240
- head_weight: bfloat16 [4096, 32768], P('grp', 'vocab'), may hold values from -0.25 to 0.25
- cluster_weight: bfloat16 [4096, 3], replicated, may hold values from -0.5 to 0.5
- proj_one: bfloat16 [4096, 1024], P('vocab'), may hold values from -0.09375 to 0.09375
- proj_two: bfloat16 [4096, 256], P('vocab'), may hold values from -0.09375 to 0.09375
- proj_three: bfloat16 [4096, 64], P('vocab'), may hold values from -0.09375 to 0.09375
- tail_one: bfloat16 [1024, 65536], P('grp', 'vocab'), may hold values from -0.5 to 0.5
- tail_two: bfloat16 [256, 65536], P('grp', 'vocab'), may hold values from -1 to 1
- tail_three: bfloat16 [64, 65536], P('grp', 'vocab'), may hold values from -2 to 2
- targets: int32 [2048], P('grp'), may hold values from 0 to 229375, as said below
- flags: int32 [2048, 3], P('grp'), may hold values from 0 to 1, as said below
Outputs:
- target_logprob: float32 [2048], P('grp')
- tail_entropy: float32 [2048, 3], P('grp')
Inputs may be any that keep to these rules, and one draw needn't show every extreme that they name: `targets`: a target at or beyond 32768 lies in tail (t - 32768) // 65536. flags[b, c] is 1 whenever the target of sequence b lies in tail c.
All inputs are finite; a program needn't handle non-finite values.
Results may differ from a plain program's by a relative error of at most 0.0092.
Values may be sent and summed in bfloat16 or wider, within the bound.
No kernel may reach another device: no remote copies, remote signals or barrier semaphores. Data moves between devices by JAX's collectives and lax.ppermute only.
A program may use at most 64 MiB of HBM per device.

v0:
```python
import functools

import jax
import jax.numpy as jnp
from jax import lax
from jax.experimental import pallas as pl
from jax.experimental.pallas import tpu as pltpu
from jax.sharding import Mesh
from jax.sharding import PartitionSpec as P


V_HEAD = 32768
TAIL = 65536
VOCAB = ("vocab_0", "vocab_1", "vocab_2")
CHIPS, CORE = VOCAB[:2], VOCAB[2]


def ring(shard, axis, cut):
    n = lax.axis_size(axis)
    up = [(i, (i + 1) % n) for i in range(n)]
    down = [(i, (i - 1) % n) for i in range(n)]
    found = {}
    right, left = shard, shard
    for step in range(1, n // 2):
        right = lax.ppermute(right, axis, up)
        left = lax.ppermute(left, axis, down)
        found[-step], found[step] = right, left
    first = lax.ppermute(right[:cut], axis, up)
    second = lax.ppermute(left[cut:], axis, down)
    return found, first, second


def copy_for_each(shard, axis):
    n = lax.psum(1, axis)
    copies = jnp.broadcast_to(shard, (n, *shard.shape))
    return lax.all_to_all(copies, axis, split_axis=0, concat_axis=0, tiled=True)


def dot(a, b):
    return jnp.dot(a, b, preferred_element_type=jnp.float32)


def kernel_call(body, out_shape, flops, scratch=(), mib=16):
    vmem = pl.BlockSpec(memory_space=pltpu.VMEM)
    smem = pl.BlockSpec(memory_space=pltpu.SMEM)

    def call(scalars, *arrays):
        return pl.pallas_call(
            body,
            out_shape=out_shape,
            in_specs=[smem] * (scalars is not None) + [vmem] * len(arrays),
            out_specs=jax.tree.map(lambda _: vmem, out_shape),
            scratch_shapes=list(scratch),
            cost_estimate=pl.CostEstimate(flops=flops, bytes_accessed=1 << 20, transcendentals=0),
            compiler_params=pltpu.CompilerParams(vmem_limit_bytes=mib << 20),
        )(*(() if scalars is None else (scalars,)), *arrays)

    return call


def project_kernel(weight_ref, hidden_ref, out_ref):
    joined = jnp.concatenate([weight_ref[k] for k in range(weight_ref.shape[0])], axis=1)
    out_ref[...] = lax.dot_general(
        joined, hidden_ref[...], (((1,), (1,)), ((), ())), preferred_element_type=jnp.float32
    ).astype(out_ref.dtype)


def spread(block, owner, count):
    tall = jnp.concatenate([block] * count, axis=0)
    row = lax.broadcasted_iota(jnp.int32, tall.shape, 0)
    return tall, row // block.shape[0] == owner


def part_kernel(h, owner_ref, turned_ref, hidden_ref, *refs):
    shard_refs = refs[: h.count - 1]
    proj_ref, head_ref, one_ref, two_ref, three_ref, wide_ref = refs[h.count - 1 :]
    proj_ref[...] = turned_ref[...].T
    n, half = h.count, h.half
    last = owner_ref[n - 1]
    blank = jnp.zeros((h.one, half), wide_ref.dtype)
    small = jnp.zeros((h.two, half), wide_ref.dtype)
    for side in range(2):
        wide_ref[side, pl.ds(pl.multiple_of(last * h.one, h.one), h.one), :] = blank
        two_ref[side, pl.ds(pl.multiple_of(last * h.two, h.two), h.two), :] = small
    threes = [jnp.zeros((h.three * n, half), jnp.float32)] * 2
    head = None
    for k, ref in enumerate(shard_refs):
        owner = owner_ref[k]
        for side in range(2):
            wide_ref[side, pl.ds(pl.multiple_of(owner * h.one, h.one), h.one), :] = ref[
                side * h.one : (side + 1) * h.one, :
            ]
            at = 2 * h.one + side * h.two
            two_ref[side, pl.ds(pl.multiple_of(owner * h.two, h.two), h.two), :] = ref[
                at : at + h.two, :
            ]
        both = ref[h.three_at : h.head_at, :].astype(jnp.float32)
        for side in range(2):
            tall, there = spread(both[side * h.three : (side + 1) * h.three], owner, n)
            threes[side] = jnp.where(there, tall, threes[side])
        features = hidden_ref[:, pl.ds(pl.multiple_of(owner * h.head, h.head), h.head)]
        term = dot(features, ref[h.head_at :, :])
        head = term if head is None else head + term
    head_ref[...] = head
    for side in range(2):
        three_ref[side] = threes[side].astype(three_ref.dtype)
        one_ref[:, side * half : (side + 1) * half] = dot(
            proj_ref[:, : h.one * n], wide_ref[side]
        )


def last_kernel(
    h,
    owner_ref,
    first_ref,
    second_ref,
    hidden_ref,
    proj_ref,
    head_ref,
    one_ref,
    two_ref,
    three_ref,
    ids_ref,
    out_ref,
    wide_ref,
):
    n, half = h.count, h.half
    owner = owner_ref[n - 1]
    rows = hidden_ref.shape[0]
    rest = h.cut - h.head_at
    at = pl.multiple_of(owner * h.head, h.head)
    head = head_ref[...] + dot(hidden_ref[:, pl.ds(at, rest)], first_ref[h.head_at :, :])
    at = pl.multiple_of(owner * h.head + rest, 128)
    head = head + dot(hidden_ref[:, pl.ds(at, h.head - rest)], second_ref[...])
    one_features = proj_ref[:, pl.ds(pl.multiple_of(owner * h.one, h.one), h.one)]
    two_features = proj_ref[:, h.one * n : (h.one + h.two) * n]
    three_features = proj_ref[:, (h.one + h.two) * n : (h.one + h.two + h.three) * n]
    wide_ref[...] = two_ref[...]
    both = first_ref[h.three_at : h.head_at, :].astype(jnp.float32)
    ones, twos, threes = [], [], []
    for side in range(2):
        ones.append(
            one_ref[:, side * half : (side + 1) * half]
            + dot(one_features, first_ref[side * h.one : (side + 1) * h.one, :])
        )
        at = 2 * h.one + side * h.two
        wide_ref[side, pl.ds(pl.multiple_of(owner * h.two, h.two), h.two), :] = first_ref[
            at : at + h.two, :
        ]
        twos.append(dot(two_features, wide_ref[side]))
        tall, there = spread(both[side * h.three : (side + 1) * h.three], owner, n)
        block = jnp.where(there, tall, three_ref[side].astype(jnp.float32))
        threes.append(dot(three_features, block.astype(three_ref.dtype)))
    columns = []
    pick = jnp.zeros((rows, 1), jnp.float32)
    tops, sums, weighted = [], [], []
    for k, sides in enumerate(([head], ones, twos, threes)):
        top = functools.reduce(
            jnp.maximum, [jnp.max(logits, axis=1, keepdims=True) for logits in sides]
        )
        total = jnp.zeros((rows, 1), jnp.float32)
        mass = jnp.zeros((rows, 1), jnp.float32)
        for side, logits in enumerate(sides):
            expo = jnp.exp(logits - top)
            total = total + jnp.sum(expo, axis=1, keepdims=True)
            if k:
                mass = mass + jnp.sum(expo * logits, axis=1, keepdims=True)
            word = lax.broadcasted_iota(jnp.int32, logits.shape, 1) + side * half
            hit = word == ids_ref[:, k : k + 1]
            pick = pick + jnp.sum(jnp.where(hit, logits, 0.0), axis=1, keepdims=True)
        tops.append(top)
        sums.append(total)
        if k:
            weighted.append(mass)
    columns = [*tops, *sums, *weighted, pick]
    lane = lax.broadcasted_iota(jnp.int32, (rows, 128), 1)
    table = jnp.zeros((rows, 128), jnp.float32)
    for k, column in enumerate(columns):
        table = jnp.where(lane == k, column, table)
    out_ref[...] = table.T[: out_ref.shape[0]]


def combined(every):
    tops = every[:, 0:4]
    top = jnp.max(tops, axis=0)
    scale = jnp.exp(tops - top)
    sums = jnp.sum(every[:, 4:8] * scale, axis=0)
    weighted = jnp.sum(every[:, 8:11] * scale[:, 1:4], axis=0)
    pick = jnp.sum(every[:, 11:12], axis=0)
    return jnp.concatenate([top, sums, weighted, pick], axis=0)


class Heights:
    def __init__(self, count, one, two, three, head, half):
        self.count, self.one, self.two, self.three = count, one, two, three
        self.head, self.half = head, half
        self.three_at = 2 * (one + two)
        self.head_at = 2 * (one + two + three)
        self.cut = self.head_at + 128


def one_device(
    hidden,
    head_weight,
    cluster_weight,
    proj_one,
    proj_two,
    proj_three,
    tail_one,
    tail_two,
    tail_three,
    targets,
    flags,
):
    rows = hidden.shape[0]
    head_cols = head_weight.shape[1]
    tail_cols = tail_one.shape[1]
    half = tail_cols // 2
    n_chips = lax.psum(1, CHIPS)
    n_grp = lax.axis_size("grp")
    core = lax.axis_index(CORE)
    vocab_index = lax.axis_index(VOCAB)
    grp_index = lax.axis_index("grp")

    tails = (tail_one, tail_two, tail_three)
    h = Heights(n_grp, *(t.shape[0] for t in tails), head_weight.shape[0], half)
    packed = jnp.concatenate(
        [part for tail in tails for part in (tail[:, :half], tail[:, half:])] + [head_weight], axis=0
    )
    found, first, second = ring(packed, "grp", h.cut)
    offsets = [0, *found, n_grp // 2]
    owners = (grp_index + jnp.array(offsets, jnp.int32)) % n_grp

    widths = (proj_one.shape[1], proj_two.shape[1], proj_three.shape[1])
    total = sum(widths)
    share = -(-total // (2 * n_chips) // 8) * 8
    joined = lax.all_gather(
        jnp.concatenate((proj_one, proj_two, proj_three), axis=1), CORE, axis=0, tiled=True
    )
    turned = jnp.pad(joined.T, ((0, 2 * n_chips * share - total), (0, 0)))
    turned = turned.reshape(2, n_chips, share, joined.shape[0])
    pieces = lax.dynamic_index_in_dim(turned, core, 0, keepdims=False)
    pieces = lax.all_to_all(pieces, CHIPS, split_axis=0, concat_axis=0, tiled=True)
    mine = kernel_call(
        project_kernel,
        jax.ShapeDtypeStruct((share, rows), jnp.bfloat16),
        2 * share * hidden.size,
    )(None, pieces, hidden)
    turned = copy_for_each(mine, CHIPS)
    turned = lax.all_gather(turned, CORE)
    turned = turned.reshape(2 * n_chips * share, rows)

    wide = jnp.bfloat16
    part_call = kernel_call(
        functools.partial(part_kernel, h),
        (
            jax.ShapeDtypeStruct((rows, turned.shape[0]), wide),
            jax.ShapeDtypeStruct((rows, head_cols), jnp.float32),
            jax.ShapeDtypeStruct((rows, tail_cols), jnp.float32),
            jax.ShapeDtypeStruct((2, h.two * n_grp, half), wide),
            jax.ShapeDtypeStruct((2, h.three * n_grp, half), wide),
        ),
        2 * rows * packed.size * n_grp,
        [pltpu.VMEM((2, h.one * n_grp, half), wide)],
    )
    part = part_call(owners, turned, hidden, packed, *found.values())

    cluster_logits = dot(hidden, cluster_weight)
    relative = targets - V_HEAD
    cluster = relative // TAIL
    word = relative - cluster * TAIL
    ids = jnp.stack(
        [targets - vocab_index * head_cols]
        + [jnp.where(cluster == k, word - vocab_index * tail_cols, -1) for k in range(3)],
        axis=1,
    )
    stats = kernel_call(
        functools.partial(last_kernel, h),
        jax.ShapeDtypeStruct((12, rows), jnp.float32),
        2 * rows * packed.size,
        [pltpu.VMEM((2, h.two * n_grp, half), wide)],
    )(owners, first, second, hidden, *part, ids)

    mid = rows // 2

    def own(array):
        return lax.dynamic_slice_in_dim(array, core * mid, mid, array.ndim - 1)

    stats = combined(own(lax.all_gather(stats, CORE)))
    stats = combined(copy_for_each(stats, CHIPS))
    scores, cluster, targets = own(cluster_logits.T), own(cluster), own(targets)
    top = jnp.maximum(stats[0], jnp.max(scores, axis=0))
    all_sum = stats[4] * jnp.exp(stats[0] - top) + jnp.sum(jnp.exp(scores - top), axis=0)
    head_lse = top + jnp.log(all_sum)
    tail_sum = stats[5:8]
    tail_lse = stats[1:4] + jnp.log(tail_sum)
    tail_mean = stats[8:11] / tail_sum
    entropy = own(flags.T).astype(jnp.float32) * (tail_lse - tail_mean)
    which = cluster[None, :] == jnp.arange(3, dtype=jnp.int32)[:, None]
    cluster_term = jnp.sum(jnp.where(which, scores - tail_lse, 0.0), axis=0)
    picked = stats[11]
    target_logprob = jnp.where(targets < V_HEAD, picked, picked + cluster_term) - head_lse
    final = lax.all_gather(
        jnp.concatenate([target_logprob[None], entropy], axis=0), CORE, axis=1, tiled=True
    )
    return (final[0], final[1:].T)


def solution(mesh):
    finer = Mesh(
        mesh.devices.reshape(8, 4, 2, mesh.shape["grp"]), ("vocab_0", "vocab_1", "vocab_2", "grp")
    )
    in_specs = (
        P("grp", None),
        P("grp", VOCAB),
        P(),
        P(VOCAB, None),
        P(VOCAB, None),
        P(VOCAB, None),
        P("grp", VOCAB),
        P("grp", VOCAB),
        P("grp", VOCAB),
        P("grp"),
        P("grp", None),
    )
    out_specs = (P("grp"), P("grp", None))
    return jax.shard_map(
        one_device, mesh=finer, in_specs=in_specs, out_specs=out_specs, check_vma=False
    )
```

profile of v0, /device:TPU:1, one launch (start us, length us, event | category | flops | bytes accessed | tf_op | source)
XLA Modules:
  0.0 135.7 jit_solution(15990596239552756594)
XLA Ops:
  0.6 0.0 copy-start
  0.6 0.9 slice_dynamic-update-slice_fusion.1
  1.6 0.9 slice_dynamic-update-slice_fusion
  2.5 0.8 slice_dynamic-update-slice_fusion.3
  3.3 0.8 slice_dynamic-update-slice_fusion.2
  4.0 0.7 constant_dynamic-update-slice_fusion.2
  4.7 0.7 constant_dynamic-update-slice_fusion.1
  5.4 1.2 constant_dynamic-update-slice_fusion.refs_0_
  6.6 4.8 %collective-permute-start = (bf16[848,512]{1,0:T(8,128)(2,1)S(1)}, bf16[848,512]{1,0:T(8,128)(2,1)S(1)}, u32[]{:S(2)}, u32[]{:S(2)}) collective-permute-start(bf16[848,512]{1,0:T(8,128)(2,1)S(1)} %constant_dynamic-update-slice_fusion.refs_0_), channel_id=1, source_target_pairs={{0,1},{1,2},{2,3},{3,4},{4,5},{5,6},{6,7},{7,0},{8,9},{9,10},{10,1... | collective-permute-start | bytes 2605064 | tf_op jit(solution)/shard_map/ppermute | solution.py:25
  11.5 8.6 %collective-permute-start.4 = (bf16[848,512]{1,0:T(8,128)(2,1)S(1)}, bf16[848,512]{1,0:T(8,128)(2,1)}, u32[]{:S(2)}, u32[]{:S(2)}) collective-permute-start(bf16[848,512]{1,0:T(8,128)(2,1)S(1)} %constant_dynamic-update-slice_fusion.refs_0_), channel_id=1, source_target_pairs={{0,7},{1,0},{2,1},{3,2},{4,3},{5,4},{6,5},{7,6},{8,15},{9,8},{10,9... | collective-permute-start | bytes 2605064 | tf_op jit(solution)/shard_map/ppermute | solution.py:26
  20.1 0.0 copy-start.2
  20.1 0.9 copy-done.2
  21.0 16.1 %collective-permute-done.refs_1_ = bf16[848,512]{1,0:T(8,128)(2,1)S(1)} collective-permute-done((bf16[848,512]{1,0:T(8,128)(2,1)S(1)}, bf16[848,512]{1,0:T(8,128)(2,1)S(1)}, u32[]{:S(2)}, u32[]{:S(2)}) %collective-permute-start) | collective-permute-done | bytes 868384 | tf_op jit(solution)/shard_map/ppermute | solution.py:25
  37.1 1.9 %collective-permute-start.1 = (bf16[848,512]{1,0:T(8,128)(2,1)S(1)}, bf16[848,512]{1,0:T(8,128)(2,1)}, u32[]{:S(2)}, u32[]{:S(2)}) collective-permute-start(bf16[848,512]{1,0:T(8,128)(2,1)S(1)} %collective-permute-done.refs_1_), channel_id=1, source_target_pairs={{0,1},{1,2},{2,3},{3,4},{4,5},{5,6},{6,7},{7,0},{8,9},{9,10},{10,1... | collective-permute-start | bytes 2605064 | tf_op jit(solution)/shard_map/ppermute | solution.py:25
  39.0 0.0 collective-permute-done.4.refs_2_
  39.0 4.6 %collective-permute-start.5 = (bf16[848,512]{1,0:T(8,128)(2,1)}, bf16[848,512]{1,0:T(8,128)(2,1)}, u32[]{:S(2)}, u32[]{:S(2)}) collective-permute-start(bf16[848,512]{1,0:T(8,128)(2,1)} %collective-permute-done.4.refs_2_), channel_id=1, source_target_pairs={{0,7},{1,0},{2,1},{3,2},{4,3},{5,4},{6,5},{7,6},{8,15},{9,8},{10,9... | collective-permute-start | bytes 2605064 | tf_op jit(solution)/shard_map/ppermute | solution.py:26
  43.6 1.0 pad_maximum_fusion
  44.6 3.5 %all_gather.18 = bf16[128,1344]{1,0:T(8,128)(2,1)S(1)} all-gather(bf16[64,1344]{1,0:T(8,128)(2,1)S(1)} %pad_maximum_fusion), channel_id=1, replica_groups=mesh['vocab_0'=8,'vocab_1'=4,'vocab_2'=2,'grp'=8] {'vocab_2'}, dimensions={0}, use_global_device_ids=true | all-gather | bytes 516096 | tf_op jit(solution)/shard_map/all_gather | solution.py:237
  48.1 0.9 copy.26
  49.0 1.0 pad.4
  50.0 0.0 copy-start.8
  50.0 0.0 copy-start.6
  50.0 0.7 dynamic-slice_bitcast_fusion
  50.7 9.7 %all-to-all-start = ((bf16[32,24,128]{2,1,0:T(8,128)(2,1)}), bf16[32,24,128]{2,1,0:T(8,128)(2,1)S(1)}, u32[]{:S(2)}, u32[]{:S(2)}) async-start(bf16[32,24,128]{2,1,0:T(8,128)(2,1)} %dynamic-slice_bitcast_fusion), calls=%async_computation | async-start | bytes 393216 | tf_op jit(solution)/shard_map/all_to_all | solution.py:243
  60.4 0.0 copy-done.4
  60.4 0.0 collective-permute-done.1.refs_3_
  60.4 1.9 %collective-permute-start.2 = (bf16[848,512]{1,0:T(8,128)(2,1)}, bf16[848,512]{1,0:T(8,128)(2,1)S(1)}, u32[]{:S(2)}, u32[]{:S(2)}) collective-permute-start(bf16[848,512]{1,0:T(8,128)(2,1)} %collective-permute-done.1.refs_3_), channel_id=1, source_target_pairs={{0,1},{1,2},{2,3},{3,4},{4,5},{5,6},{6,7},{7,0},{8,9},{9,10},{10,1... | collective-permute-start | bytes 2605064 | tf_op jit(solution)/shard_map/ppermute | solution.py:25
  62.4 0.0 collective-permute-done.5.refs_4_
  62.4 4.6 %collective-permute-start.6 = (bf16[848,512]{1,0:T(8,128)(2,1)}, bf16[848,512]{1,0:T(8,128)(2,1)}, u32[]{:S(2)}, u32[]{:S(2)}) collective-permute-start(bf16[848,512]{1,0:T(8,128)(2,1)} %collective-permute-done.5.refs_4_), channel_id=1, source_target_pairs={{0,7},{1,0},{2,1},{3,2},{4,3},{5,4},{6,5},{7,6},{8,15},{9,8},{10,9... | collective-permute-start | bytes 2605064 | tf_op jit(solution)/shard_map/ppermute | solution.py:26
  67.0 4.0 %all-to-all-done.weight_ref = bf16[32,24,128]{2,1,0:T(8,128)(2,1)S(1)} async-done(((bf16[32,24,128]{2,1,0:T(8,128)(2,1)}), bf16[32,24,128]{2,1,0:T(8,128)(2,1)S(1)}, u32[]{:S(2)}, u32[]{:S(2)}) %all-to-all-start) | async-done | bytes 196640 | tf_op jit(solution)/shard_map/all_to_all | solution.py:243
  71.0 0.0 copy-done.1
  71.0 0.7 shard_map.131
  71.7 0.8 broadcast_in_dim.22
  72.5 5.3 %all-to-all-start.1 = ((bf16[32,24,256]{2,1,0:T(8,128)(2,1)}), bf16[32,24,256]{2,1,0:T(8,128)(2,1)}, u32[]{:S(2)}, u32[]{:S(2)}) async-start(bf16[32,24,256]{2,1,0:T(8,128)(2,1)} %broadcast_in_dim.22), calls=%async_computation.1 | async-start | bytes 786432 | tf_op jit(solution)/shard_map/all_to_all | solution.py:36
  77.8 0.0 copy-done.8
  77.9 0.0 copy-done.6
  77.9 5.1 %collective-permute-done.2.refs_5_ = bf16[848,512]{1,0:T(8,128)(2,1)S(1)} collective-permute-done((bf16[848,512]{1,0:T(8,128)(2,1)}, bf16[848,512]{1,0:T(8,128)(2,1)S(1)}, u32[]{:S(2)}, u32[]{:S(2)}) %collective-permute-start.2) | collective-permute-done | bytes 868384 | tf_op jit(solution)/shard_map/ppermute | solution.py:25
  83.0 0.8 slice.97
  83.8 1.9 %collective-permute-start.3 = (bf16[464,512]{1,0:T(8,128)(2,1)}, bf16[464,512]{1,0:T(8,128)(2,1)}, u32[]{:S(2)}, u32[]{:S(2)}) collective-permute-start(bf16[464,512]{1,0:T(8,128)(2,1)} %slice.97), channel_id=1, source_target_pairs={{0,1},{1,2},{2,3},{3,4},{4,5},{5,6},{6,7},{7,0},{8,9},{9,10},{10,1... | collective-permute-start | bytes 1425416 | tf_op jit(solution)/shard_map/ppermute | solution.py:28
  85.8 0.0 collective-permute-done.6.refs_6_
  85.8 1.8 %slice.98 = bf16[384,512]{1,0:T(8,128)(2,1)} slice(bf16[848,512]{1,0:T(8,128)(2,1)} %collective-permute-done.6.refs_6_), slice={[464:848], [0:512]} | slice | bytes 786432 | tf_op jit(solution)/shard_map/slice | solution.py:29
  87.5 4.6 %collective-permute-start.7 = (bf16[384,512]{1,0:T(8,128)(2,1)}, bf16[384,512]{1,0:T(8,128)(2,1)S(1)}, u32[]{:S(2)}, u32[]{:S(2)}) collective-permute-start(bf16[384,512]{1,0:T(8,128)(2,1)} %slice.98), channel_id=1, source_target_pairs={{0,7},{1,0},{2,1},{3,2},{4,3},{5,4},{6,5},{7,6},{8,15},{9,8},{10,9... | collective-permute-start | bytes 1179656 | tf_op jit(solution)/shard_map/ppermute | solution.py:29
  92.1 0.1 copy.27.ids_ref
  92.3 0.0 all-to-all-done.1
  92.3 5.2 %all-gather = bf16[64,24,256]{2,1,0:T(8,128)(2,1)S(1)} all-gather(bf16[32,24,256]{2,1,0:T(8,128)(2,1)} %all-to-all-done.1), channel_id=2, replica_groups=mesh['vocab_0'=8,'vocab_1'=4,'vocab_2'=2,'grp'=8] {'vocab_2'}, dimensions={0}, use_global_device_ids=true | all-gather | bytes 1179648 | tf_op jit(solution)/shard_map/all_gather | solution.py:250
  97.5 1.2 copy-done.3
  98.7 1.2 copy-done.5
  99.8 3.8 %shard_map.132 = (bf16[256,1536]{1,0:T(8,128)(2,1)S(1)}, f32[256,512]{1,0:T(8,128)S(1)}, f32[256,1024]{1,0:T(8,128)S(1)}, bf16[2,256,512]{2,1,0:T(8,128)(2,1)S(1)}, bf16[2,64,512]{2,1,0:T(8,128)(2,1)S(1)}) custom-call(s32[8]{0:T(128)S(1)} %and_select_fusion.1.owner_ref, bf16[1536,256]{1,0:T(8,128)(2,1)S(1)} %bitcast.50, bf16[256,4096]{1,0:T(8,128)(2,1)S(1)} %copy-done.1, ...), custom_call_target="tpu_custom_call" | custom-call | flops 1778384896 | bytes 1048576 | tf_op jit(solution)/shard_map/pallas_call | solution.py:48
  103.6 0.0 collective-permute-done.7.second_ref
  103.6 0.0 collective-permute-done.3.first_ref
  103.6 3.0 %shard_map.133 = f32[12,256]{1,0:T(8,128)S(1)} custom-call(s32[8]{0:T(128)S(1)} %and_select_fusion.1.owner_ref, bf16[464,512]{1,0:T(8,128)(2,1)} %collective-permute-done.3.first_ref, bf16[384,512]{1,0:T(8,128)(2,1)S(1)} %collective-permute-done.7.second_ref, bf16[256,4096]{1,0:T(8,128)(2,1)S(1)} %copy-done.1, ...), custom_call_target="tpu_custom_call" | custom-call | flops 222298112 | bytes 1048576 | tf_op jit(solution)/shard_map/pallas_call | solution.py:48
  106.6 2.0 %all-gather.2 = f32[2,12,256]{2,1,0:T(8,128)S(1)} all-gather(f32[1,12,256]{2,1,0:T(8,128)S(1)} %bitcast.51), channel_id=3, replica_groups=mesh['vocab_0'=8,'vocab_1'=4,'vocab_2'=2,'grp'=8] {'vocab_2'}, dimensions={0}, use_global_device_ids=true | all-gather | bytes 36864 | tf_op jit(solution)/shard_map/all_gather | solution.py:289
  108.6 0.1 fusion.5
  108.7 0.1 fusion.3
  108.8 0.7 broadcast_in_dim.23
  109.6 9.2 %all-to-all-start.2 = ((f32[32,12,128]{2,1,0:T(8,128)}), f32[32,12,128]{2,1,0:T(8,128)S(1)}, u32[]{:S(2)}, u32[]{:S(2)}) async-start(f32[32,12,128]{2,1,0:T(8,128)} %broadcast_in_dim.23), calls=%async_computation.2 | async-start | bytes 524288 | tf_op jit(solution)/shard_map/all_to_all | solution.py:36
  118.8 0.1 dynamic_slice.22
  118.9 0.6 fusion.14
  119.5 10.9 %all-to-all-done.2 = f32[32,12,128]{2,1,0:T(8,128)S(1)} async-done(((f32[32,12,128]{2,1,0:T(8,128)}), f32[32,12,128]{2,1,0:T(8,128)S(1)}, u32[]{:S(2)}, u32[]{:S(2)}) %all-to-all-start.2) | async-done | bytes 196640 | tf_op jit(solution)/shard_map/all_to_all | solution.py:36
  130.5 0.1 fusion.1
  130.7 0.1 fusion.13
  130.8 3.8 %all_gather.23 = f32[4,256]{1,0:T(4,128)S(1)} all-gather(f32[4,128]{1,0:T(4,128)S(1)} %pad_maximum_fusion.2), channel_id=1, replica_groups=mesh['vocab_0'=8,'vocab_1'=4,'vocab_2'=2,'grp'=8] {'vocab_2'}, dimensions={1}, use_global_device_ids=true | all-gather | bytes 6144 | tf_op jit(solution)/shard_map/all_gather | solution.py:303
  134.6 0.6 slice_bitcast_fusion
  135.1 0.6 slice.105
  (22 shorter events, 0.3 us)
Async XLA Ops:
  0.6 118.3 %copy-start = (bf16[4096,3]{0,1:T(4,128)(2,1)S(1)}, bf16[4096,3]{0,1:T(4,128)(2,1)}, u32[]{:S(2)}) copy-start(bf16[4096,3]{0,1:T(4,128)(2,1)} %param.14) | copy-start | bytes 73732
  5.4 65.6 %copy-start.1 = (bf16[256,4096]{1,0:T(8,128)(2,1)S(1)}, bf16[256,4096]{1,0:T(8,128)(2,1)}, u32[]{:S(2)}) copy-start(bf16[256,4096]{1,0:T(8,128)(2,1)} %hidden_ref.5) | copy-start | bytes 6291460
  6.6 30.5 %collective-permute-start = (bf16[848,512]{1,0:T(8,128)(2,1)S(1)}, bf16[848,512]{1,0:T(8,128)(2,1)S(1)}, u32[]{:S(2)}, u32[]{:S(2)}) collective-permute-start(bf16[848,512]{1,0:T(8,128)(2,1)S(1)} %constant_dynamic-update-slice_fusion.refs_0_), channel_id=1, source_target_pairs={{0,1},{1,2},{2,3},{3,4},{4,5},{5,6},{6,7},{7,0},{8,9},{9,10},{10,1... | collective-permute-start | bytes 2605064 | tf_op jit(solution)/shard_map/ppermute | solution.py:25
  11.5 27.6 %collective-permute-start.4 = (bf16[848,512]{1,0:T(8,128)(2,1)S(1)}, bf16[848,512]{1,0:T(8,128)(2,1)}, u32[]{:S(2)}, u32[]{:S(2)}) collective-permute-start(bf16[848,512]{1,0:T(8,128)(2,1)S(1)} %constant_dynamic-update-slice_fusion.refs_0_), channel_id=1, source_target_pairs={{0,7},{1,0},{2,1},{3,2},{4,3},{5,4},{6,5},{7,6},{8,15},{9,8},{10,9... | collective-permute-start | bytes 2605064 | tf_op jit(solution)/shard_map/ppermute | solution.py:26
  20.1 0.9 copy-start.2
  37.1 23.3 %copy-start.4 = (bf16[848,512]{1,0:T(8,128)(2,1)}, bf16[848,512]{1,0:T(8,128)(2,1)S(1)}, u32[]{:S(2)}) copy-start(bf16[848,512]{1,0:T(8,128)(2,1)S(1)} %collective-permute-done.refs_1_) | copy-start | bytes 2605060
  37.1 23.3 %collective-permute-start.1 = (bf16[848,512]{1,0:T(8,128)(2,1)S(1)}, bf16[848,512]{1,0:T(8,128)(2,1)}, u32[]{:S(2)}, u32[]{:S(2)}) collective-permute-start(bf16[848,512]{1,0:T(8,128)(2,1)S(1)} %collective-permute-done.refs_1_), channel_id=1, source_target_pairs={{0,1},{1,2},{2,3},{3,4},{4,5},{5,6},{6,7},{7,0},{8,9},{9,10},{10,1... | collective-permute-start | bytes 2605064 | tf_op jit(solution)/shard_map/ppermute | solution.py:25
  39.0 23.3 %collective-permute-start.5 = (bf16[848,512]{1,0:T(8,128)(2,1)}, bf16[848,512]{1,0:T(8,128)(2,1)}, u32[]{:S(2)}, u32[]{:S(2)}) collective-permute-start(bf16[848,512]{1,0:T(8,128)(2,1)} %collective-permute-done.4.refs_2_), channel_id=1, source_target_pairs={{0,7},{1,0},{2,1},{3,2},{4,3},{5,4},{6,5},{7,6},{8,15},{9,8},{10,9... | collective-permute-start | bytes 2605064 | tf_op jit(solution)/shard_map/ppermute | solution.py:26
  50.0 27.8 %copy-start.8 = (s32[8]{0:T(128)S(1)}, s32[8]{0:T(128)}, u32[]{:S(2)}) copy-start(s32[8]{0:T(128)} %constant.82.clone) | copy-start | bytes 100
  50.0 27.8 %copy-start.6 = (s32[256]{0:T(256)S(1)}, s32[256]{0:T(256)}, u32[]{:S(2)}) copy-start(s32[256]{0:T(256)} %param.21) | copy-start | bytes 3076
  50.7 20.3 %all-to-all-start = ((bf16[32,24,128]{2,1,0:T(8,128)(2,1)}), bf16[32,24,128]{2,1,0:T(8,128)(2,1)S(1)}, u32[]{:S(2)}, u32[]{:S(2)}) async-start(bf16[32,24,128]{2,1,0:T(8,128)(2,1)} %dynamic-slice_bitcast_fusion), calls=%async_computation | async-start | bytes 393216 | tf_op jit(solution)/shard_map/all_to_all | solution.py:243
  60.4 22.6 %collective-permute-start.2 = (bf16[848,512]{1,0:T(8,128)(2,1)}, bf16[848,512]{1,0:T(8,128)(2,1)S(1)}, u32[]{:S(2)}, u32[]{:S(2)}) collective-permute-start(bf16[848,512]{1,0:T(8,128)(2,1)} %collective-permute-done.1.refs_3_), channel_id=1, source_target_pairs={{0,1},{1,2},{2,3},{3,4},{4,5},{5,6},{6,7},{7,0},{8,9},{9,10},{10,1... | collective-permute-start | bytes 2605064 | tf_op jit(solution)/shard_map/ppermute | solution.py:25
  62.4 23.4 %collective-permute-start.6 = (bf16[848,512]{1,0:T(8,128)(2,1)}, bf16[848,512]{1,0:T(8,128)(2,1)}, u32[]{:S(2)}, u32[]{:S(2)}) collective-permute-start(bf16[848,512]{1,0:T(8,128)(2,1)} %collective-permute-done.5.refs_4_), channel_id=1, source_target_pairs={{0,7},{1,0},{2,1},{3,2},{4,3},{5,4},{6,5},{7,6},{8,15},{9,8},{10,9... | collective-permute-start | bytes 2605064 | tf_op jit(solution)/shard_map/ppermute | solution.py:26
  72.5 19.8 %all-to-all-start.1 = ((bf16[32,24,256]{2,1,0:T(8,128)(2,1)}), bf16[32,24,256]{2,1,0:T(8,128)(2,1)}, u32[]{:S(2)}, u32[]{:S(2)}) async-start(bf16[32,24,256]{2,1,0:T(8,128)(2,1)} %broadcast_in_dim.22), calls=%async_computation.1 | async-start | bytes 786432 | tf_op jit(solution)/shard_map/all_to_all | solution.py:36
  83.8 19.8 %collective-permute-start.3 = (bf16[464,512]{1,0:T(8,128)(2,1)}, bf16[464,512]{1,0:T(8,128)(2,1)}, u32[]{:S(2)}, u32[]{:S(2)}) collective-permute-start(bf16[464,512]{1,0:T(8,128)(2,1)} %slice.97), channel_id=1, source_target_pairs={{0,1},{1,2},{2,3},{3,4},{4,5},{5,6},{6,7},{7,0},{8,9},{9,10},{10,1... | collective-permute-start | bytes 1425416 | tf_op jit(solution)/shard_map/ppermute | solution.py:28
  87.5 16.1 %collective-permute-start.7 = (bf16[384,512]{1,0:T(8,128)(2,1)}, bf16[384,512]{1,0:T(8,128)(2,1)S(1)}, u32[]{:S(2)}, u32[]{:S(2)}) collective-permute-start(bf16[384,512]{1,0:T(8,128)(2,1)} %slice.98), channel_id=1, source_target_pairs={{0,7},{1,0},{2,1},{3,2},{4,3},{5,4},{6,5},{7,6},{8,15},{9,8},{10,9... | collective-permute-start | bytes 1179656 | tf_op jit(solution)/shard_map/ppermute | solution.py:29
  97.5 1.2 copy-start.3
  98.7 1.2 copy-start.5
  106.6 23.9 %copy-start.7 = (s32[256,3]{0,1:T(4,128)S(1)}, s32[256,3]{0,1:T(4,128)}, u32[]{:S(2)}) copy-start(s32[256,3]{0,1:T(4,128)} %param.22) | copy-start | bytes 9220
  109.6 20.9 %all-to-all-start.2 = ((f32[32,12,128]{2,1,0:T(8,128)}), f32[32,12,128]{2,1,0:T(8,128)S(1)}, u32[]{:S(2)}, u32[]{:S(2)}) async-start(f32[32,12,128]{2,1,0:T(8,128)} %broadcast_in_dim.23), calls=%async_computation.2 | async-start | bytes 524288 | tf_op jit(solution)/shard_map/all_to_all | solution.py:36
where the time goes:
time: 137 us; the launch traced here: 136 us
  starting transfers between devices  57.1 us (42%)
  waiting for transfers between devices  36.2 us (26%)
  local copies, waits for them, and re-layouts  17.3 us (13%)
  blocking collectives  14.5 us (11%)
  Pallas kernels  7.51 us (5%)
  other arithmetic  1.54 us (1%)
    ppermute x3, waiting for transfers between devices, ring(): right = lax.ppermute(right, axis, up)  21.3 us
    ppermute x3, starting transfers between devices, ring(): left = lax.ppermute(left, axis, down)  17.7 us
    all_to_all x2, starting transfers between devices, copy_for_each(): return lax.all_to_all(copies, axis, split_axis=0, concat_axis=0, tiled=True)  14.6 us
    all_to_all x2, waiting for transfers between devices, copy_for_each(): return lax.all_to_all(copies, axis, split_axis=0, concat_axis=0, tiled=True)  10.9 us
    all_to_all x1, starting transfers between devices, one_device(): lax.all_to_all(pieces, CHIPS, split_axis=0, concat_axis=0, tiled=True)  9.67 us
    ppermute x3, starting transfers between devices, ring(): right = lax.ppermute(right, axis, up)  8.65 us
    unnamed x24, local copies, waits for them, and re-layouts  8.01 us
    pallas_call x3, Pallas kernels, call(): pl.pallas_call(body, out_shape=out_shape, in_specs=[smem] * (scalars is n...  7.51 us
  transfers between devices with their start and end apart: 11, of which 4 were waited for; matrix products, arithmetic and copies ran while one was open for 6% of the time, Pallas kernels for 3%

commit v1 on v0

--- a/solution.py
+++ b/solution.py
@@ -56,6 +56,39 @@
         )(*(() if scalars is None else (scalars,)), *arrays)
 
     return call
+
+
+def pack_kernel(places, *refs):
+    sources, out_ref, sems = refs[:-2], refs[-2], refs[-1]
+    copies = []
+    for k, (source, left, at) in enumerate(places):
+        ref = sources[source]
+        copies.append(
+            pltpu.make_async_copy(
+                ref.at[:, pl.ds(left, out_ref.shape[1])],
+                out_ref.at[pl.ds(at, ref.shape[0]), :],
+                sems.at[k],
+            )
+        )
+    for copy in copies:
+        copy.start()
+    for copy in copies:
+        copy.wait()
+
+
+def packed_rows(sources, width):
+    places, at = [], 0
+    for k, source in enumerate(sources):
+        for left in range(0, source.shape[1], width):
+            places.append((k, left, at))
+            at += source.shape[0]
+    return pl.pallas_call(
+        functools.partial(pack_kernel, places),
+        out_shape=jax.ShapeDtypeStruct((at, width), sources[0].dtype),
+        in_specs=[pl.BlockSpec(memory_space=pltpu.HBM)] * len(sources),
+        out_specs=pl.BlockSpec(memory_space=pltpu.VMEM),
+        scratch_shapes=[pltpu.SemaphoreType.DMA((len(places),))],
+    )(*sources)
 
 
 def project_kernel(weight_ref, hidden_ref, out_ref):
@@ -180,14 +213,46 @@
     out_ref[...] = table.T[: out_ref.shape[0]]
 
 
-def combined(every):
-    tops = every[:, 0:4]
-    top = jnp.max(tops, axis=0)
-    scale = jnp.exp(tops - top)
-    sums = jnp.sum(every[:, 4:8] * scale, axis=0)
-    weighted = jnp.sum(every[:, 8:11] * scale[:, 1:4], axis=0)
-    pick = jnp.sum(every[:, 11:12], axis=0)
-    return jnp.concatenate([top, sums, weighted, pick], axis=0)
+def combined(rows, axis):
+    def down(combine, array):
+        return combine(array, axis=axis, keepdims=True)
+
+    tops = [down(jnp.max, row) for row in rows[0:4]]
+    scales = [jnp.exp(row - top) for row, top in zip(rows[0:4], tops)]
+    sums = [down(jnp.sum, row * scale) for row, scale in zip(rows[4:8], scales)]
+    masses = [down(jnp.sum, row * scale) for row, scale in zip(rows[8:11], scales[1:])]
+    return [*tops, *sums, *masses, down(jnp.sum, rows[11])]
+
+
+def merge_kernel(core_ref, stats_ref, out_ref):
+    mid = stats_ref.shape[2] // 2
+    lanes = pl.ds(pl.multiple_of(core_ref[0] * mid, mid), mid)
+    both = [stats_ref[core, :, lanes] for core in range(2)]
+    rows = [jnp.concatenate([table[k : k + 1] for table in both], axis=0) for k in range(12)]
+    for k, row in enumerate(combined(rows, 0)):
+        out_ref[:, 0, k * mid : (k + 1) * mid] = jnp.broadcast_to(row, (out_ref.shape[0], mid))
+
+
+def finish_kernel(core_ref, stats_ref, scores_ref, flags_ref, targets_ref, out_ref):
+    mid = out_ref.shape[1]
+    lanes = pl.ds(pl.multiple_of(core_ref[0] * mid, mid), mid)
+    rows = combined([stats_ref[:, 0, k * mid : (k + 1) * mid] for k in range(12)], 0)
+    scores, flags = scores_ref[:, lanes], flags_ref[:, lanes]
+    targets = targets_ref[:, lanes]
+    top = jnp.maximum(rows[0], jnp.max(scores, axis=0, keepdims=True))
+    total = rows[4] * jnp.exp(rows[0] - top) + jnp.sum(
+        jnp.exp(scores - top), axis=0, keepdims=True
+    )
+    head_lse = top + jnp.log(total)
+    picked = rows[11]
+    for k in range(3):
+        lse = rows[1 + k] + jnp.log(rows[5 + k])
+        mean = rows[8 + k] / rows[5 + k]
+        out_ref[1 + k : 2 + k, :] = flags[k : k + 1].astype(jnp.float32) * (lse - mean)
+        low = V_HEAD + k * TAIL
+        inside = jnp.logical_and(targets >= low, targets < low + TAIL)
+        picked = picked + jnp.where(inside, scores[k : k + 1] - lse, 0.0)
+    out_ref[0:1, :] = picked - head_lse
 
 
 class Heights:
@@ -224,9 +289,7 @@
 
     tails = (tail_one, tail_two, tail_three)
     h = Heights(n_grp, *(t.shape[0] for t in tails), head_weight.shape[0], half)
-    packed = jnp.concatenate(
-        [part for tail in tails for part in (tail[:, :half], tail[:, half:])] + [head_weight], axis=0
-    )
+    packed = packed_rows((*tails, head_weight), half)
     found, first, second = ring(packed, "grp", h.cut)
     offsets = [0, *found, n_grp // 2]
     owners = (grp_index + jnp.array(offsets, jnp.int32)) % n_grp
@@ -282,27 +345,15 @@
     )(owners, first, second, hidden, *part, ids)
 
     mid = rows // 2
-
-    def own(array):
-        return lax.dynamic_slice_in_dim(array, core * mid, mid, array.ndim - 1)
-
-    stats = combined(own(lax.all_gather(stats, CORE)))
-    stats = combined(copy_for_each(stats, CHIPS))
-    scores, cluster, targets = own(cluster_logits.T), own(cluster), own(targets)
-    top = jnp.maximum(stats[0], jnp.max(scores, axis=0))
-    all_sum = stats[4] * jnp.exp(stats[0] - top) + jnp.sum(jnp.exp(scores - top), axis=0)
-    head_lse = top + jnp.log(all_sum)
-    tail_sum = stats[5:8]
-    tail_lse = stats[1:4] + jnp.log(tail_sum)
-    tail_mean = stats[8:11] / tail_sum
-    entropy = own(flags.T).astype(jnp.float32) * (tail_lse - tail_mean)
-    which = cluster[None, :] == jnp.arange(3, dtype=jnp.int32)[:, None]
-    cluster_term = jnp.sum(jnp.where(which, scores - tail_lse, 0.0), axis=0)
-    picked = stats[11]
-    target_logprob = jnp.where(targets < V_HEAD, picked, picked + cluster_term) - head_lse
-    final = lax.all_gather(
-        jnp.concatenate([target_logprob[None], entropy], axis=0), CORE, axis=1, tiled=True
-    )
+    which = jnp.reshape(core, (1,)).astype(jnp.int32)
+    copies = kernel_call(
+        merge_kernel, jax.ShapeDtypeStruct((n_chips, 1, 12 * mid), jnp.float32), 1 << 20, mib=4
+    )(which, lax.all_gather(stats, CORE))
+    copies = lax.all_to_all(copies, CHIPS, split_axis=0, concat_axis=0, tiled=True)
+    final = kernel_call(
+        finish_kernel, jax.ShapeDtypeStruct((4, mid), jnp.float32), 1 << 20, mib=4
+    )(which, copies, cluster_logits.T, flags.T, targets[None])
+    final = lax.all_gather(final, CORE, axis=1, tiled=True)
     return (final[0], final[1:].T)
 
 

time: 137 us -> 132 us (0.964)
  local copies, waits for them, and re-layouts: 17.3 us -> 9.57 us
  Pallas kernels: 7.51 us -> 11.2 us
    all_to_all x2 -> x1, waiting for transfers between devices: 10.9 us -> 0.01 us  [copy_for_each(): return lax.all_to_all(copies, axis, split_axis=0, concat_axis=0, tiled=True)]
    all_to_all x0 -> x1, waiting for transfers between devices: none -> 9.91 us  [one_device(): lax.all_to_all(copies, CHIPS, split_axis=0, concat_axis=0, tiled=True)]
    all_to_all x2 -> x1, starting transfers between devices: 14.6 us -> 5.31 us  [copy_for_each(): return lax.all_to_all(copies, axis, split_axis=0, concat_axis=0, tiled=True)]
    all_to_all x0 -> x1, starting transfers between devices: none -> 9.22 us  [one_device(): lax.all_to_all(copies, CHIPS, split_axis=0, concat_axis=0, tiled=True)]
    unnamed x24 -> x16, local copies, waits for them, and re-layouts: 8.01 us -> 1.21 us
    pallas_call x0 -> x1, Pallas kernels: none -> 2.4 us  [packed_rows(): pl.pallas_call(functools.partial(pack_kernel, places), out_shape=jax.Shap...]
    pallas_call x3 -> x5, Pallas kernels: 7.51 us -> 8.79 us  [call(): pl.pallas_call(body, out_shape=out_shape, in_specs=[smem] * (scalars is n...]
  transfers between devices with their start and end apart: 11 -> 11, of which waited for: 4 -> 4; matrix products, arithmetic and copies ran while one was open for 6% -> 7% of each run, Pallas kernels for 3% -> 4%
where the time goes in v1:
time: 132 us; the launch traced here: 131 us
  starting transfers between devices  57.1 us (43%)
  waiting for transfers between devices  36.4 us (28%)
  blocking collectives  14.2 us (11%)
  Pallas kernels  11.2 us (8%)
  local copies, waits for them, and re-layouts  9.57 us (7%)
    ppermute x3, waiting for transfers between devices, ring(): right = lax.ppermute(right, axis, up)  22.5 us
    ppermute x3, starting transfers between devices, ring(): left = lax.ppermute(left, axis, down)  17.7 us
    all_to_all x1, waiting for transfers between devices, one_device(): lax.all_to_all(copies, CHIPS, split_axis=0, concat_axis=0, tiled=True)  9.91 us
    all_to_all x1, starting transfers between devices, one_device(): lax.all_to_all(pieces, CHIPS, split_axis=0, concat_axis=0, tiled=True)  9.67 us
    all_to_all x1, starting transfers between devices, one_device(): lax.all_to_all(copies, CHIPS, split_axis=0, concat_axis=0, tiled=True)  9.22 us
    pallas_call x5, Pallas kernels, call(): pl.pallas_call(body, out_shape=out_shape, in_specs=[smem] * (scalars is n...  8.79 us
    ppermute x3, starting transfers between devices, ring(): right = lax.ppermute(right, axis, up)  8.65 us
    all_to_all x1, starting transfers between devices, copy_for_each(): return lax.all_to_all(copies, axis, split_axis=0, concat_axis=0, tiled=True)  5.31 us
  transfers between devices with their start and end apart: 11, of which 4 were waited for; matrix products, arithmetic and copies ran while one was open for 7% of the time, Pallas kernels for 4%

profile of v1, /device:TPU:1, one launch (start us, length us, event | category | flops | bytes accessed | tf_op | source)
XLA Modules:
  0.0 131.0 jit_solution(4550956449983413801)
XLA Ops:
  0.6 0.0 copy-start
  0.6 0.0 copy-start.1
  0.7 2.4 %shard_map.131.refs_0_ = bf16[848,512]{1,0:T(8,128)(2,1)} custom-call(bf16[128,1024]{1,0:T(8,128)(2,1)} %refs_0_.1, bf16[32,1024]{1,0:T(8,128)(2,1)} %refs_1_.1, bf16[8,1024]{1,0:T(8,128)(2,1)} %refs_2_.1, bf16[512,512]{1,0:T(8,128)(2,1)} %refs_3_.1), custom_call_target="tpu_custom_call" | custom-call | tf_op jit(solution)/shard_map/pallas_call | solution.py:85
  3.1 4.8 %collective-permute-start = (bf16[848,512]{1,0:T(8,128)(2,1)}, bf16[848,512]{1,0:T(8,128)(2,1)S(1)}, u32[]{:S(2)}, u32[]{:S(2)}) collective-permute-start(bf16[848,512]{1,0:T(8,128)(2,1)} %shard_map.131.refs_0_), channel_id=1, source_target_pairs={{0,1},{1,2},{2,3},{3,4},{4,5},{5,6},{6,7},{7,0},{8,9},{9,10},{10,1... | collective-permute-start | bytes 2605064 | tf_op jit(solution)/shard_map/ppermute | solution.py:25
  7.9 8.6 %collective-permute-start.4 = (bf16[848,512]{1,0:T(8,128)(2,1)}, bf16[848,512]{1,0:T(8,128)(2,1)}, u32[]{:S(2)}, u32[]{:S(2)}) collective-permute-start(bf16[848,512]{1,0:T(8,128)(2,1)} %shard_map.131.refs_0_), channel_id=1, source_target_pairs={{0,7},{1,0},{2,1},{3,2},{4,3},{5,4},{6,5},{7,6},{8,15},{9,8},{10,9... | collective-permute-start | bytes 2605064 | tf_op jit(solution)/shard_map/ppermute | solution.py:26
  16.5 17.3 %collective-permute-done.refs_1_ = bf16[848,512]{1,0:T(8,128)(2,1)S(1)} collective-permute-done((bf16[848,512]{1,0:T(8,128)(2,1)}, bf16[848,512]{1,0:T(8,128)(2,1)S(1)}, u32[]{:S(2)}, u32[]{:S(2)}) %collective-permute-start) | collective-permute-done | bytes 868384 | tf_op jit(solution)/shard_map/ppermute | solution.py:25
  33.8 0.0 copy-start.3
  33.8 1.9 %collective-permute-start.1 = (bf16[848,512]{1,0:T(8,128)(2,1)S(1)}, bf16[848,512]{1,0:T(8,128)(2,1)}, u32[]{:S(2)}, u32[]{:S(2)}) collective-permute-start(bf16[848,512]{1,0:T(8,128)(2,1)S(1)} %collective-permute-done.refs_1_), channel_id=1, source_target_pairs={{0,1},{1,2},{2,3},{3,4},{4,5},{5,6},{6,7},{7,0},{8,9},{9,10},{10,1... | collective-permute-start | bytes 2605064 | tf_op jit(solution)/shard_map/ppermute | solution.py:25
  35.7 0.0 collective-permute-done.4.refs_2_
  35.7 4.6 %collective-permute-start.5 = (bf16[848,512]{1,0:T(8,128)(2,1)}, bf16[848,512]{1,0:T(8,128)(2,1)}, u32[]{:S(2)}, u32[]{:S(2)}) collective-permute-start(bf16[848,512]{1,0:T(8,128)(2,1)} %collective-permute-done.4.refs_2_), channel_id=1, source_target_pairs={{0,7},{1,0},{2,1},{3,2},{4,3},{5,4},{6,5},{7,6},{8,15},{9,8},{10,9... | collective-permute-start | bytes 2605064 | tf_op jit(solution)/shard_map/ppermute | solution.py:26
  40.3 1.0 pad_maximum_fusion
  41.2 3.5 %all_gather.18 = bf16[128,1344]{1,0:T(8,128)(2,1)S(1)} all-gather(bf16[64,1344]{1,0:T(8,128)(2,1)S(1)} %pad_maximum_fusion), channel_id=1, replica_groups=mesh['vocab_0'=8,'vocab_1'=4,'vocab_2'=2,'grp'=8] {'vocab_2'}, dimensions={0}, use_global_device_ids=true | all-gather | bytes 516096 | tf_op jit(solution)/shard_map/all_gather | solution.py:300
  44.7 0.9 copy.22
  45.7 1.0 pad.4
  46.7 0.0 copy-start.7
  46.7 0.0 copy-start.5
  46.7 0.7 dynamic-slice_bitcast_fusion
  47.4 9.7 %all-to-all-start = ((bf16[32,24,128]{2,1,0:T(8,128)(2,1)}), bf16[32,24,128]{2,1,0:T(8,128)(2,1)S(1)}, u32[]{:S(2)}, u32[]{:S(2)}) async-start(bf16[32,24,128]{2,1,0:T(8,128)(2,1)} %dynamic-slice_bitcast_fusion), calls=%async_computation | async-start | bytes 393216 | tf_op jit(solution)/shard_map/all_to_all | solution.py:306
  57.1 0.0 collective-permute-done.1.refs_3_
  57.1 1.9 %collective-permute-start.2 = (bf16[848,512]{1,0:T(8,128)(2,1)}, bf16[848,512]{1,0:T(8,128)(2,1)}, u32[]{:S(2)}, u32[]{:S(2)}) collective-permute-start(bf16[848,512]{1,0:T(8,128)(2,1)} %collective-permute-done.1.refs_3_), channel_id=1, source_target_pairs={{0,1},{1,2},{2,3},{3,4},{4,5},{5,6},{6,7},{7,0},{8,9},{9,10},{10,1... | collective-permute-start | bytes 2605064 | tf_op jit(solution)/shard_map/ppermute | solution.py:25
  59.0 0.0 collective-permute-done.5.refs_4_
  59.0 4.6 %collective-permute-start.6 = (bf16[848,512]{1,0:T(8,128)(2,1)}, bf16[848,512]{1,0:T(8,128)(2,1)}, u32[]{:S(2)}, u32[]{:S(2)}) collective-permute-start(bf16[848,512]{1,0:T(8,128)(2,1)} %collective-permute-done.5.refs_4_), channel_id=1, source_target_pairs={{0,7},{1,0},{2,1},{3,2},{4,3},{5,4},{6,5},{7,6},{8,15},{9,8},{10,9... | collective-permute-start | bytes 2605064 | tf_op jit(solution)/shard_map/ppermute | solution.py:26
  63.6 4.0 %all-to-all-done.weight_ref = bf16[32,24,128]{2,1,0:T(8,128)(2,1)S(1)} async-done(((bf16[32,24,128]{2,1,0:T(8,128)(2,1)}), bf16[32,24,128]{2,1,0:T(8,128)(2,1)S(1)}, u32[]{:S(2)}, u32[]{:S(2)}) %all-to-all-start) | async-done | bytes 196640 | tf_op jit(solution)/shard_map/all_to_all | solution.py:306
  67.7 0.0 copy-done.3
  67.7 0.0 copy-done.1
  67.7 0.7 shard_map.132
  68.4 0.0 copy-start.2
  68.4 0.8 broadcast_in_dim.10
  69.2 5.3 %all-to-all-start.1 = ((bf16[32,24,256]{2,1,0:T(8,128)(2,1)}), bf16[32,24,256]{2,1,0:T(8,128)(2,1)}, u32[]{:S(2)}, u32[]{:S(2)}) async-start(bf16[32,24,256]{2,1,0:T(8,128)(2,1)} %broadcast_in_dim.10), calls=%async_computation.1 | async-start | bytes 786432 | tf_op jit(solution)/shard_map/all_to_all | solution.py:36
  74.5 0.0 copy-done.7
  74.6 0.0 copy-done.5
  74.6 5.2 %collective-permute-done.2.refs_5_ = bf16[848,512]{1,0:T(8,128)(2,1)} collective-permute-done((bf16[848,512]{1,0:T(8,128)(2,1)}, bf16[848,512]{1,0:T(8,128)(2,1)}, u32[]{:S(2)}, u32[]{:S(2)}) %collective-permute-start.2) | collective-permute-done | bytes 868384 | tf_op jit(solution)/shard_map/ppermute | solution.py:25
  79.8 1.9 %slice.16 = bf16[464,512]{1,0:T(8,128)(2,1)} slice(bf16[848,512]{1,0:T(8,128)(2,1)} %collective-permute-done.2.refs_5_), slice={[0:464], [0:512]} | slice | bytes 950272 | tf_op jit(solution)/shard_map/slice | solution.py:28
  81.7 1.9 %collective-permute-start.3 = (bf16[464,512]{1,0:T(8,128)(2,1)}, bf16[464,512]{1,0:T(8,128)(2,1)}, u32[]{:S(2)}, u32[]{:S(2)}) collective-permute-start(bf16[464,512]{1,0:T(8,128)(2,1)} %slice.16), channel_id=1, source_target_pairs={{0,1},{1,2},{2,3},{3,4},{4,5},{5,6},{6,7},{7,0},{8,9},{9,10},{10,1... | collective-permute-start | bytes 1425416 | tf_op jit(solution)/shard_map/ppermute | solution.py:28
  83.6 0.0 collective-permute-done.6.refs_6_
  83.6 1.8 %slice.17 = bf16[384,512]{1,0:T(8,128)(2,1)} slice(bf16[848,512]{1,0:T(8,128)(2,1)} %collective-permute-done.6.refs_6_), slice={[464:848], [0:512]} | slice | bytes 786432 | tf_op jit(solution)/shard_map/slice | solution.py:29
  85.4 4.6 %collective-permute-start.7 = (bf16[384,512]{1,0:T(8,128)(2,1)}, bf16[384,512]{1,0:T(8,128)(2,1)S(1)}, u32[]{:S(2)}, u32[]{:S(2)}) collective-permute-start(bf16[384,512]{1,0:T(8,128)(2,1)} %slice.17), channel_id=1, source_target_pairs={{0,7},{1,0},{2,1},{3,2},{4,3},{5,4},{6,5},{7,6},{8,15},{9,8},{10,9... | collective-permute-start | bytes 1179656 | tf_op jit(solution)/shard_map/ppermute | solution.py:29
  89.9 0.1 copy.23.ids_ref
  90.1 0.0 all-to-all-done.1
  90.1 5.2 %all-gather = bf16[64,24,256]{2,1,0:T(8,128)(2,1)S(1)} all-gather(bf16[32,24,256]{2,1,0:T(8,128)(2,1)} %all-to-all-done.1), channel_id=2, replica_groups=mesh['vocab_0'=8,'vocab_1'=4,'vocab_2'=2,'grp'=8] {'vocab_2'}, dimensions={0}, use_global_device_ids=true | all-gather | bytes 1179648 | tf_op jit(solution)/shard_map/all_gather | solution.py:313
  95.3 0.0 copy-done.2
  95.3 0.0 copy-start.4
  95.3 1.2 copy-done.4
  96.4 4.1 %shard_map.133 = (bf16[256,1536]{1,0:T(8,128)(2,1)S(1)}, f32[256,512]{1,0:T(8,128)S(1)}, f32[256,1024]{1,0:T(8,128)S(1)}, bf16[2,256,512]{2,1,0:T(8,128)(2,1)S(1)}, bf16[2,64,512]{2,1,0:T(8,128)(2,1)S(1)}) custom-call(s32[8]{0:T(128)S(1)} %and_select_fusion.1.owner_ref, bf16[1536,256]{1,0:T(8,128)(2,1)S(1)} %bitcast.18, bf16[256,4096]{1,0:T(8,128)(2,1)S(1)} %copy-done.1, ...), custom_call_target="tpu_custom_call" | custom-call | flops 1778384896 | bytes 1048576 | tf_op jit(solution)/shard_map/pallas_call | solution.py:48
  100.5 0.0 collective-permute-done.7.second_ref
  100.5 0.0 collective-permute-done.3.first_ref
  100.5 3.1 %shard_map.134 = f32[12,256]{1,0:T(8,128)S(1)} custom-call(s32[8]{0:T(128)S(1)} %and_select_fusion.1.owner_ref, bf16[464,512]{1,0:T(8,128)(2,1)} %collective-permute-done.3.first_ref, bf16[384,512]{1,0:T(8,128)(2,1)S(1)} %collective-permute-done.7.second_ref, bf16[256,4096]{1,0:T(8,128)(2,1)S(1)} %copy-done.1, ...), custom_call_target="tpu_custom_call" | custom-call | flops 222298112 | bytes 1048576 | tf_op jit(solution)/shard_map/pallas_call | solution.py:48
  103.6 0.0 copy-start.6
  103.6 2.0 %all-gather.2.stats_ref = f32[2,12,256]{2,1,0:T(8,128)S(1)} all-gather(f32[1,12,256]{2,1,0:T(8,128)S(1)} %bitcast.19), channel_id=3, replica_groups=mesh['vocab_0'=8,'vocab_1'=4,'vocab_2'=2,'grp'=8] {'vocab_2'}, dimensions={0}, use_global_device_ids=true | all-gather | bytes 36864 | tf_op jit(solution)/shard_map/all_gather | solution.py:351
  105.6 0.8 shard_map.135
  106.4 9.2 %all-to-all-start.2 = ((f32[32,1,1536]{2,1,0:T(1,128)}), f32[32,1,1536]{2,1,0:T(1,128)S(1)}, u32[]{:S(2)}, u32[]{:S(2)}) async-start(f32[32,1,1536]{2,1,0:T(1,128)} %shard_map.135), calls=%async_computation.2 | async-start | bytes 393216 | tf_op jit(solution)/shard_map/all_to_all | solution.py:352
  115.6 0.0 copy-done
  115.6 0.6 fusion.1.scores_ref
  116.3 9.9 %all-to-all-done.2.stats_ref = f32[32,1,1536]{2,1,0:T(1,128)S(1)} async-done(((f32[32,1,1536]{2,1,0:T(1,128)}), f32[32,1,1536]{2,1,0:T(1,128)S(1)}, u32[]{:S(2)}, u32[]{:S(2)}) %all-to-all-start.2) | async-done | bytes 196640 | tf_op jit(solution)/shard_map/all_to_all | solution.py:352
  126.2 0.0 copy-done.6
  126.2 0.2 shard_map.136
  126.3 3.5 %all_gather.23 = f32[4,256]{1,0:T(4,128)S(1)} all-gather(f32[4,128]{1,0:T(4,128)S(1)} %shard_map.136), channel_id=1, replica_groups=mesh['vocab_0'=8,'vocab_1'=4,'vocab_2'=2,'grp'=8] {'vocab_2'}, dimensions={1}, use_global_device_ids=true | all-gather | bytes 6144 | tf_op jit(solution)/shard_map/all_gather | solution.py:356
  129.8 0.6 slice_bitcast_fusion
  130.4 0.6 slice.18
  (4 shorter events, 0.1 us)
Async XLA Ops:
  0.6 115.0 %copy-start = (bf16[4096,3]{0,1:T(4,128)(2,1)S(1)}, bf16[4096,3]{0,1:T(4,128)(2,1)}, u32[]{:S(2)}) copy-start(bf16[4096,3]{0,1:T(4,128)(2,1)} %param.14) | copy-start | bytes 73732
  0.6 67.0 %copy-start.1 = (bf16[256,4096]{1,0:T(8,128)(2,1)S(1)}, bf16[256,4096]{1,0:T(8,128)(2,1)}, u32[]{:S(2)}) copy-start(bf16[256,4096]{1,0:T(8,128)(2,1)} %hidden_ref.5) | copy-start | bytes 6291460
  3.1 30.7 %collective-permute-start = (bf16[848,512]{1,0:T(8,128)(2,1)}, bf16[848,512]{1,0:T(8,128)(2,1)S(1)}, u32[]{:S(2)}, u32[]{:S(2)}) collective-permute-start(bf16[848,512]{1,0:T(8,128)(2,1)} %shard_map.131.refs_0_), channel_id=1, source_target_pairs={{0,1},{1,2},{2,3},{3,4},{4,5},{5,6},{6,7},{7,0},{8,9},{9,10},{10,1... | collective-permute-start | bytes 2605064 | tf_op jit(solution)/shard_map/ppermute | solution.py:25
  7.9 27.8 %collective-permute-start.4 = (bf16[848,512]{1,0:T(8,128)(2,1)}, bf16[848,512]{1,0:T(8,128)(2,1)}, u32[]{:S(2)}, u32[]{:S(2)}) collective-permute-start(bf16[848,512]{1,0:T(8,128)(2,1)} %shard_map.131.refs_0_), channel_id=1, source_target_pairs={{0,7},{1,0},{2,1},{3,2},{4,3},{5,4},{6,5},{7,6},{8,15},{9,8},{10,9... | collective-permute-start | bytes 2605064 | tf_op jit(solution)/shard_map/ppermute | solution.py:26
  33.8 33.9 %copy-start.3 = (bf16[848,512]{1,0:T(8,128)(2,1)}, bf16[848,512]{1,0:T(8,128)(2,1)S(1)}, u32[]{:S(2)}) copy-start(bf16[848,512]{1,0:T(8,128)(2,1)S(1)} %collective-permute-done.refs_1_) | copy-start | bytes 2605060
  33.8 23.3 %collective-permute-start.1 = (bf16[848,512]{1,0:T(8,128)(2,1)S(1)}, bf16[848,512]{1,0:T(8,128)(2,1)}, u32[]{:S(2)}, u32[]{:S(2)}) collective-permute-start(bf16[848,512]{1,0:T(8,128)(2,1)S(1)} %collective-permute-done.refs_1_), channel_id=1, source_target_pairs={{0,1},{1,2},{2,3},{3,4},{4,5},{5,6},{6,7},{7,0},{8,9},{9,10},{10,1... | collective-permute-start | bytes 2605064 | tf_op jit(solution)/shard_map/ppermute | solution.py:25
  35.7 23.3 %collective-permute-start.5 = (bf16[848,512]{1,0:T(8,128)(2,1)}, bf16[848,512]{1,0:T(8,128)(2,1)}, u32[]{:S(2)}, u32[]{:S(2)}) collective-permute-start(bf16[848,512]{1,0:T(8,128)(2,1)} %collective-permute-done.4.refs_2_), channel_id=1, source_target_pairs={{0,7},{1,0},{2,1},{3,2},{4,3},{5,4},{6,5},{7,6},{8,15},{9,8},{10,9... | collective-permute-start | bytes 2605064 | tf_op jit(solution)/shard_map/ppermute | solution.py:26
  46.7 27.9 %copy-start.7 = (s32[8]{0:T(128)S(1)}, s32[8]{0:T(128)}, u32[]{:S(2)}) copy-start(s32[8]{0:T(128)} %constant.72.clone) | copy-start | bytes 100
  46.7 27.9 %copy-start.5 = (s32[256]{0:T(256)S(1)}, s32[256]{0:T(256)}, u32[]{:S(2)}) copy-start(s32[256]{0:T(256)} %param.21) | copy-start | bytes 3076
  47.4 20.3 %all-to-all-start = ((bf16[32,24,128]{2,1,0:T(8,128)(2,1)}), bf16[32,24,128]{2,1,0:T(8,128)(2,1)S(1)}, u32[]{:S(2)}, u32[]{:S(2)}) async-start(bf16[32,24,128]{2,1,0:T(8,128)(2,1)} %dynamic-slice_bitcast_fusion), calls=%async_computation | async-start | bytes 393216 | tf_op jit(solution)/shard_map/all_to_all | solution.py:306
  57.1 22.7 %collective-permute-start.2 = (bf16[848,512]{1,0:T(8,128)(2,1)}, bf16[848,512]{1,0:T(8,128)(2,1)}, u32[]{:S(2)}, u32[]{:S(2)}) collective-permute-start(bf16[848,512]{1,0:T(8,128)(2,1)} %collective-permute-done.1.refs_3_), channel_id=1, source_target_pairs={{0,1},{1,2},{2,3},{3,4},{4,5},{5,6},{6,7},{7,0},{8,9},{9,10},{10,1... | collective-permute-start | bytes 2605064 | tf_op jit(solution)/shard_map/ppermute | solution.py:25
  59.0 24.6 %collective-permute-start.6 = (bf16[848,512]{1,0:T(8,128)(2,1)}, bf16[848,512]{1,0:T(8,128)(2,1)}, u32[]{:S(2)}, u32[]{:S(2)}) collective-permute-start(bf16[848,512]{1,0:T(8,128)(2,1)} %collective-permute-done.5.refs_4_), channel_id=1, source_target_pairs={{0,7},{1,0},{2,1},{3,2},{4,3},{5,4},{6,5},{7,6},{8,15},{9,8},{10,9... | collective-permute-start | bytes 2605064 | tf_op jit(solution)/shard_map/ppermute | solution.py:26
  68.4 26.9 %copy-start.2 = (bf16[848,512]{1,0:T(8,128)(2,1)S(1)}, bf16[848,512]{1,0:T(8,128)(2,1)}, u32[]{:S(2)}) copy-start(bf16[848,512]{1,0:T(8,128)(2,1)} %shard_map.131.refs_0_) | copy-start | bytes 2605060
  69.2 20.9 %all-to-all-start.1 = ((bf16[32,24,256]{2,1,0:T(8,128)(2,1)}), bf16[32,24,256]{2,1,0:T(8,128)(2,1)}, u32[]{:S(2)}, u32[]{:S(2)}) async-start(bf16[32,24,256]{2,1,0:T(8,128)(2,1)} %broadcast_in_dim.10), calls=%async_computation.1 | async-start | bytes 786432 | tf_op jit(solution)/shard_map/all_to_all | solution.py:36
  81.7 18.9 %collective-permute-start.3 = (bf16[464,512]{1,0:T(8,128)(2,1)}, bf16[464,512]{1,0:T(8,128)(2,1)}, u32[]{:S(2)}, u32[]{:S(2)}) collective-permute-start(bf16[464,512]{1,0:T(8,128)(2,1)} %slice.16), channel_id=1, source_target_pairs={{0,1},{1,2},{2,3},{3,4},{4,5},{5,6},{6,7},{7,0},{8,9},{9,10},{10,1... | collective-permute-start | bytes 1425416 | tf_op jit(solution)/shard_map/ppermute | solution.py:28
  85.4 15.2 %collective-permute-start.7 = (bf16[384,512]{1,0:T(8,128)(2,1)}, bf16[384,512]{1,0:T(8,128)(2,1)S(1)}, u32[]{:S(2)}, u32[]{:S(2)}) collective-permute-start(bf16[384,512]{1,0:T(8,128)(2,1)} %slice.17), channel_id=1, source_target_pairs={{0,7},{1,0},{2,1},{3,2},{4,3},{5,4},{6,5},{7,6},{8,15},{9,8},{10,9... | collective-permute-start | bytes 1179656 | tf_op jit(solution)/shard_map/ppermute | solution.py:29
  95.3 1.2 copy-start.4
  103.6 22.6 %copy-start.6 = (s32[256,3]{0,1:T(4,128)S(1)}, s32[256,3]{0,1:T(4,128)}, u32[]{:S(2)}) copy-start(s32[256,3]{0,1:T(4,128)} %param.22) | copy-start | bytes 9220
  106.4 19.8 %all-to-all-start.2 = ((f32[32,1,1536]{2,1,0:T(1,128)}), f32[32,1,1536]{2,1,0:T(1,128)S(1)}, u32[]{:S(2)}, u32[]{:S(2)}) async-start(f32[32,1,1536]{2,1,0:T(1,128)} %shard_map.135), calls=%async_computation.2 | async-start | bytes 393216 | tf_op jit(solution)/shard_map/all_to_all | solution.py:352

commit v2 on v1

--- a/solution.py
+++ b/solution.py
@@ -17,17 +17,22 @@
 
 def ring(shard, axis, cut):
     n = lax.axis_size(axis)
-    up = [(i, (i + 1) % n) for i in range(n)]
-    down = [(i, (i - 1) % n) for i in range(n)]
-    found = {}
-    right, left = shard, shard
+    even = [(i, i ^ 1) for i in range(n)]
+    odd = [(i, ((i + 1) ^ 1) - 1 if 0 < i < n - 1 else n - 1 - i) for i in range(n)]
+    side = 1 - 2 * (lax.axis_index(axis) % 2)
+    found, offsets = [], [0]
+    one, two = shard, shard
     for step in range(1, n // 2):
-        right = lax.ppermute(right, axis, up)
-        left = lax.ppermute(left, axis, down)
-        found[-step], found[step] = right, left
-    first = lax.ppermute(right[:cut], axis, up)
-    second = lax.ppermute(left[cut:], axis, down)
-    return found, first, second
+        before = one
+        one = lax.ppermute(two, axis, even)
+        two = lax.ppermute(before, axis, odd)
+        found += [one, two]
+        offsets += [side * step, -side * step]
+    first = lax.ppermute(two[:cut], axis, even)
+    second = lax.ppermute(one[cut:], axis, odd)
+    offsets.append(n // 2)
+    owners = (lax.axis_index(axis) + jnp.stack([jnp.int32(k) for k in offsets])) % n
+    return found, first, second, owners
 
 
 def copy_for_each(shard, axis):
@@ -210,12 +215,23 @@
     table = jnp.zeros((rows, 128), jnp.float32)
     for k, column in enumerate(columns):
         table = jnp.where(lane == k, column, table)
-    out_ref[...] = table.T[: out_ref.shape[0]]
-
-
-def combined(rows, axis):
+    write_copies(table.T, out_ref)
+
+
+def write_copies(table, out_ref):
+    width = out_ref.shape[2] // 12
+    for k in range(12):
+        out_ref[:, 0, k * width : (k + 1) * width] = jnp.broadcast_to(
+            table[k : k + 1], (out_ref.shape[0], width)
+        )
+
+
+def combined(ref):
+    width = ref.shape[2] // 12
+    rows = [ref[:, 0, k * width : (k + 1) * width] for k in range(12)]
+
     def down(combine, array):
-        return combine(array, axis=axis, keepdims=True)
+        return combine(array, axis=0, keepdims=True)
 
     tops = [down(jnp.max, row) for row in rows[0:4]]
     scales = [jnp.exp(row - top) for row, top in zip(rows[0:4], tops)]
@@ -224,21 +240,13 @@
     return [*tops, *sums, *masses, down(jnp.sum, rows[11])]
 
 
-def merge_kernel(core_ref, stats_ref, out_ref):
-    mid = stats_ref.shape[2] // 2
-    lanes = pl.ds(pl.multiple_of(core_ref[0] * mid, mid), mid)
-    both = [stats_ref[core, :, lanes] for core in range(2)]
-    rows = [jnp.concatenate([table[k : k + 1] for table in both], axis=0) for k in range(12)]
-    for k, row in enumerate(combined(rows, 0)):
-        out_ref[:, 0, k * mid : (k + 1) * mid] = jnp.broadcast_to(row, (out_ref.shape[0], mid))
-
-
-def finish_kernel(core_ref, stats_ref, scores_ref, flags_ref, targets_ref, out_ref):
-    mid = out_ref.shape[1]
-    lanes = pl.ds(pl.multiple_of(core_ref[0] * mid, mid), mid)
-    rows = combined([stats_ref[:, 0, k * mid : (k + 1) * mid] for k in range(12)], 0)
-    scores, flags = scores_ref[:, lanes], flags_ref[:, lanes]
-    targets = targets_ref[:, lanes]
+def merge_kernel(stats_ref, out_ref):
+    write_copies(jnp.concatenate(combined(stats_ref), axis=0), out_ref)
+
+
+def finish_kernel(stats_ref, scores_ref, flags_ref, targets_ref, prob_ref, entropy_ref):
+    rows = combined(stats_ref)
+    scores, flags, targets = scores_ref[...], flags_ref[...], targets_ref[...]
     top = jnp.maximum(rows[0], jnp.max(scores, axis=0, keepdims=True))
     total = rows[4] * jnp.exp(rows[0] - top) + jnp.sum(
         jnp.exp(scores - top), axis=0, keepdims=True
@@ -248,11 +256,11 @@
     for k in range(3):
         lse = rows[1 + k] + jnp.log(rows[5 + k])
         mean = rows[8 + k] / rows[5 + k]
-        out_ref[1 + k : 2 + k, :] = flags[k : k + 1].astype(jnp.float32) * (lse - mean)
+        entropy_ref[k : k + 1, :] = flags[k : k + 1].astype(jnp.float32) * (lse - mean)
         low = V_HEAD + k * TAIL
         inside = jnp.logical_and(targets >= low, targets < low + TAIL)
         picked = picked + jnp.where(inside, scores[k : k + 1] - lse, 0.0)
-    out_ref[0:1, :] = picked - head_lse
+    prob_ref[...] = picked - head_lse
 
 
 class Heights:
@@ -285,14 +293,11 @@
     n_grp = lax.axis_size("grp")
     core = lax.axis_index(CORE)
     vocab_index = lax.axis_index(VOCAB)
-    grp_index = lax.axis_index("grp")
 
     tails = (tail_one, tail_two, tail_three)
     h = Heights(n_grp, *(t.shape[0] for t in tails), head_weight.shape[0], half)
     packed = packed_rows((*tails, head_weight), half)
-    found, first, second = ring(packed, "grp", h.cut)
-    offsets = [0, *found, n_grp // 2]
-    owners = (grp_index + jnp.array(offsets, jnp.int32)) % n_grp
+    found, first, second, owners = ring(packed, "grp", h.cut)
 
     widths = (proj_one.shape[1], proj_two.shape[1], proj_three.shape[1])
     total = sum(widths)
@@ -326,7 +331,7 @@
         2 * rows * packed.size * n_grp,
         [pltpu.VMEM((2, h.one * n_grp, half), wide)],
     )
-    part = part_call(owners, turned, hidden, packed, *found.values())
+    part = part_call(owners, turned, hidden, packed, *found)
 
     cluster_logits = dot(hidden, cluster_weight)
     relative = targets - V_HEAD
@@ -337,24 +342,30 @@
         + [jnp.where(cluster == k, word - vocab_index * tail_cols, -1) for k in range(3)],
         axis=1,
     )
+    near = VOCAB[1:]
+    n_near = lax.psum(1, near)
+    n_far = lax.axis_size(VOCAB[0])
     stats = kernel_call(
         functools.partial(last_kernel, h),
-        jax.ShapeDtypeStruct((12, rows), jnp.float32),
+        jax.ShapeDtypeStruct((n_near, 1, 12 * rows), jnp.float32),
         2 * rows * packed.size,
         [pltpu.VMEM((2, h.two * n_grp, half), wide)],
     )(owners, first, second, hidden, *part, ids)
-
-    mid = rows // 2
-    which = jnp.reshape(core, (1,)).astype(jnp.int32)
-    copies = kernel_call(
-        merge_kernel, jax.ShapeDtypeStruct((n_chips, 1, 12 * mid), jnp.float32), 1 << 20, mib=4
-    )(which, lax.all_gather(stats, CORE))
-    copies = lax.all_to_all(copies, CHIPS, split_axis=0, concat_axis=0, tiled=True)
-    final = kernel_call(
-        finish_kernel, jax.ShapeDtypeStruct((4, mid), jnp.float32), 1 << 20, mib=4
-    )(which, copies, cluster_logits.T, flags.T, targets[None])
-    final = lax.all_gather(final, CORE, axis=1, tiled=True)
-    return (final[0], final[1:].T)
+    stats = lax.all_to_all(stats, near, split_axis=0, concat_axis=0, tiled=True)
+    stats = kernel_call(
+        merge_kernel, jax.ShapeDtypeStruct((n_far, 1, 12 * rows), jnp.float32), 1 << 20, mib=4
+    )(None, stats)
+    stats = lax.all_to_all(stats, VOCAB[0], split_axis=0, concat_axis=0, tiled=True)
+    target_logprob, entropy = kernel_call(
+        finish_kernel,
+        (
+            jax.ShapeDtypeStruct((1, rows), jnp.float32),
+            jax.ShapeDtypeStruct((3, rows), jnp.float32),
+        ),
+        1 << 20,
+        mib=4,
+    )(None, stats, cluster_logits.T, flags.T, targets[None])
+    return (target_logprob[0], entropy.T)
 
 
 def solution(mesh):

time: 132 us -> 129 us (0.977)
  starting transfers between devices: 57.1 us -> 49 us
  blocking collectives: 14.2 us -> 19 us
    all_to_all x0 -> x1, blocking collectives: none -> 10.7 us  [one_device(): stats = lax.all_to_all(stats, near, split_axis=0, concat_axis=0, tiled=True)]
    all_gather x2 -> x0, blocking collectives: 5.48 us -> none  [the longest x1 3.5 us: one_device(): final = lax.all_gather(final, CORE, axis=1, tiled=True)]
    ppermute x8, starting transfers between devices: 32.9 us -> 28.5 us  [the longest x3 18.2 us: ring(): two = lax.ppermute(before, axis, odd)]
    all_to_all x1, starting transfers between devices: 9.22 us -> 6.18 us  [one_device(): lax.all_to_all(stats, VOCAB[0], split_axis=0, concat_axis=0, tiled=True)]
    all_to_all x1, waiting for transfers between devices: 9.91 us -> 7.04 us  [one_device(): lax.all_to_all(stats, VOCAB[0], split_axis=0, concat_axis=0, tiled=True)]
    ppermute x8, waiting for transfers between devices: 22.5 us -> 25.1 us  [the longest x3 24.1 us: ring(): two = lax.ppermute(before, axis, odd)]
    slice x3 -> x2, local copies, waits for them, and re-layouts: 4.17 us -> 3.61 us  [the longest x1 1.85 us: ring(): first = lax.ppermute(two[:cut], axis, even)]
  transfers between devices with their start and end apart: 11 -> 11, of which waited for: 4 -> 5; matrix products, arithmetic and copies ran while one was open for 7% -> 7% of each run, Pallas kernels for 4% -> 4%
where the time goes in v2:
time: 129 us; the launch traced here: 128 us
  starting transfers between devices  49 us (38%)
  waiting for transfers between devices  37.2 us (29%)
  blocking collectives  19 us (15%)
  Pallas kernels  11.7 us (9%)
  local copies, waits for them, and re-layouts  8.5 us (7%)
    ppermute x3, waiting for transfers between devices, ring(): two = lax.ppermute(before, axis, odd)  24.1 us
    ppermute x3, starting transfers between devices, ring(): two = lax.ppermute(before, axis, odd)  18.2 us
    all_to_all x1, blocking collectives, one_device(): stats = lax.all_to_all(stats, near, split_axis=0, concat_axis=0, tiled=True)  10.7 us
    all_to_all x1, starting transfers between devices, one_device(): lax.all_to_all(pieces, CHIPS, split_axis=0, concat_axis=0, tiled=True)  9.67 us
    pallas_call x5, Pallas kernels, call(): pl.pallas_call(body, out_shape=out_shape, in_specs=[smem] * (scalars is n...  9.3 us
    all_to_all x1, waiting for transfers between devices, one_device(): lax.all_to_all(stats, VOCAB[0], split_axis=0, concat_axis=0, tiled=True)  7.04 us
    all_to_all x1, starting transfers between devices, one_device(): lax.all_to_all(stats, VOCAB[0], split_axis=0, concat_axis=0, tiled=True)  6.18 us
    ppermute x3, starting transfers between devices, ring(): one = lax.ppermute(two, axis, even)  5.75 us
  transfers between devices with their start and end apart: 11, of which 5 were waited for; matrix products, arithmetic and copies ran while one was open for 7% of the time, Pallas kernels for 4%

profile of v2, /device:TPU:1, one launch (start us, length us, event | category | flops | bytes accessed | tf_op | source)
XLA Modules:
  0.0 128.0 jit_solution(10868314127068912329)
XLA Ops:
  0.6 0.0 copy-start
  0.6 0.0 copy-start.1
  0.7 2.4 %shard_map.122.refs_0_ = bf16[848,512]{1,0:T(8,128)(2,1)} custom-call(bf16[128,1024]{1,0:T(8,128)(2,1)} %refs_0_.1, bf16[32,1024]{1,0:T(8,128)(2,1)} %refs_1_.1, bf16[8,1024]{1,0:T(8,128)(2,1)} %refs_2_.1, bf16[512,512]{1,0:T(8,128)(2,1)} %refs_3_.1), custom_call_target="tpu_custom_call" | custom-call | tf_op jit(solution)/shard_map/pallas_call | solution.py:90
  3.1 11.5 %collective-permute-start = (bf16[848,512]{1,0:T(8,128)(2,1)}, bf16[848,512]{1,0:T(8,128)(2,1)S(1)}, u32[]{:S(2)}, u32[]{:S(2)}) collective-permute-start(bf16[848,512]{1,0:T(8,128)(2,1)} %shard_map.122.refs_0_), channel_id=1, source_target_pairs={{0,7},{1,2},{2,1},{3,4},{4,3},{5,6},{6,5},{7,0},{8,15},{9,10},{10,... | collective-permute-start | bytes 2605064 | tf_op jit(solution)/shard_map/ppermute | solution.py:28
  14.6 1.9 %collective-permute-start.4 = (bf16[848,512]{1,0:T(8,128)(2,1)}, bf16[848,512]{1,0:T(8,128)(2,1)}, u32[]{:S(2)}, u32[]{:S(2)}) collective-permute-start(bf16[848,512]{1,0:T(8,128)(2,1)} %shard_map.122.refs_0_), channel_id=1, source_target_pairs={{0,1},{1,0},{2,3},{3,2},{4,5},{5,4},{6,7},{7,6},{8,9},{9,8},{10,11... | collective-permute-start | bytes 2605064 | tf_op jit(solution)/shard_map/ppermute | solution.py:27
  16.5 17.3 %collective-permute-done.refs_2_ = bf16[848,512]{1,0:T(8,128)(2,1)S(1)} collective-permute-done((bf16[848,512]{1,0:T(8,128)(2,1)}, bf16[848,512]{1,0:T(8,128)(2,1)S(1)}, u32[]{:S(2)}, u32[]{:S(2)}) %collective-permute-start) | collective-permute-done | bytes 868384 | tf_op jit(solution)/shard_map/ppermute | solution.py:28
  33.8 0.0 copy-start.3
  33.8 1.9 %collective-permute-start.1 = (bf16[848,512]{1,0:T(8,128)(2,1)S(1)}, bf16[848,512]{1,0:T(8,128)(2,1)}, u32[]{:S(2)}, u32[]{:S(2)}) collective-permute-start(bf16[848,512]{1,0:T(8,128)(2,1)S(1)} %collective-permute-done.refs_2_), channel_id=1, source_target_pairs={{0,1},{1,0},{2,3},{3,2},{4,5},{5,4},{6,7},{7,6},{8,9},{9,8},{10,11... | collective-permute-start | bytes 2605064 | tf_op jit(solution)/shard_map/ppermute | solution.py:27
  35.7 1.0 collective-permute-done.4.refs_1_
  36.7 3.3 %collective-permute-start.5 = (bf16[848,512]{1,0:T(8,128)(2,1)}, bf16[848,512]{1,0:T(8,128)(2,1)}, u32[]{:S(2)}, u32[]{:S(2)}) collective-permute-start(bf16[848,512]{1,0:T(8,128)(2,1)} %collective-permute-done.4.refs_1_), channel_id=1, source_target_pairs={{0,7},{1,2},{2,1},{3,4},{4,3},{5,6},{6,5},{7,0},{8,15},{9,10},{10,... | collective-permute-start | bytes 2605064 | tf_op jit(solution)/shard_map/ppermute | solution.py:28
  40.0 1.0 pad_maximum_fusion
  41.0 3.5 %all_gather.9 = bf16[128,1344]{1,0:T(8,128)(2,1)S(1)} all-gather(bf16[64,1344]{1,0:T(8,128)(2,1)S(1)} %pad_maximum_fusion), channel_id=1, replica_groups=mesh['vocab_0'=8,'vocab_1'=4,'vocab_2'=2,'grp'=8] {'vocab_2'}, dimensions={0}, use_global_device_ids=true | all-gather | bytes 516096 | tf_op jit(solution)/shard_map/all_gather | solution.py:305
  44.5 0.9 copy.21
  45.4 1.0 pad.4
  46.4 0.0 copy-start.5
  46.4 0.7 dynamic-slice_bitcast_fusion
  47.1 9.7 %all-to-all-start = ((bf16[32,24,128]{2,1,0:T(8,128)(2,1)}), bf16[32,24,128]{2,1,0:T(8,128)(2,1)S(1)}, u32[]{:S(2)}, u32[]{:S(2)}) async-start(bf16[32,24,128]{2,1,0:T(8,128)(2,1)} %dynamic-slice_bitcast_fusion), calls=%async_computation | async-start | bytes 393216 | tf_op jit(solution)/shard_map/all_to_all | solution.py:311
  56.8 0.0 collective-permute-done.1.refs_3_
  56.8 3.5 %collective-permute-start.2 = (bf16[848,512]{1,0:T(8,128)(2,1)}, bf16[848,512]{1,0:T(8,128)(2,1)}, u32[]{:S(2)}, u32[]{:S(2)}) collective-permute-start(bf16[848,512]{1,0:T(8,128)(2,1)} %collective-permute-done.1.refs_3_), channel_id=1, source_target_pairs={{0,7},{1,2},{2,1},{3,4},{4,3},{5,6},{6,5},{7,0},{8,15},{9,10},{10,... | collective-permute-start | bytes 2605064 | tf_op jit(solution)/shard_map/ppermute | solution.py:28
  60.3 0.0 collective-permute-done.5.refs_4_
  60.3 1.9 %collective-permute-start.6 = (bf16[848,512]{1,0:T(8,128)(2,1)}, bf16[848,512]{1,0:T(8,128)(2,1)}, u32[]{:S(2)}, u32[]{:S(2)}) collective-permute-start(bf16[848,512]{1,0:T(8,128)(2,1)} %collective-permute-done.5.refs_4_), channel_id=1, source_target_pairs={{0,1},{1,0},{2,3},{3,2},{4,5},{5,4},{6,7},{7,6},{8,9},{9,8},{10,11... | collective-permute-start | bytes 2605064 | tf_op jit(solution)/shard_map/ppermute | solution.py:27
  62.2 0.1 stack.42
  62.3 5.1 %all-to-all-done.weight_ref = bf16[32,24,128]{2,1,0:T(8,128)(2,1)S(1)} async-done(((bf16[32,24,128]{2,1,0:T(8,128)(2,1)}), bf16[32,24,128]{2,1,0:T(8,128)(2,1)S(1)}, u32[]{:S(2)}, u32[]{:S(2)}) %all-to-all-start) | async-done | bytes 196640 | tf_op jit(solution)/shard_map/all_to_all | solution.py:311
  67.4 0.0 copy-done.3
  67.4 0.0 copy-done.1
  67.4 0.7 shard_map.123
  68.1 0.0 copy-start.2
  68.1 0.8 broadcast_in_dim.10
  68.9 4.6 %all-to-all-start.1 = ((bf16[32,24,256]{2,1,0:T(8,128)(2,1)}), bf16[32,24,256]{2,1,0:T(8,128)(2,1)}, u32[]{:S(2)}, u32[]{:S(2)}) async-start(bf16[32,24,256]{2,1,0:T(8,128)(2,1)} %broadcast_in_dim.10), calls=%async_computation.1 | async-start | bytes 786432 | tf_op jit(solution)/shard_map/all_to_all | solution.py:41
  73.5 0.0 copy-done.5
  73.6 6.8 %collective-permute-done.2.refs_6_ = bf16[848,512]{1,0:T(8,128)(2,1)} collective-permute-done((bf16[848,512]{1,0:T(8,128)(2,1)}, bf16[848,512]{1,0:T(8,128)(2,1)}, u32[]{:S(2)}, u32[]{:S(2)}) %collective-permute-start.2) | collective-permute-done | bytes 868384 | tf_op jit(solution)/shard_map/ppermute | solution.py:28
  80.4 1.9 %slice.8 = bf16[464,512]{1,0:T(8,128)(2,1)} slice(bf16[848,512]{1,0:T(8,128)(2,1)} %collective-permute-done.2.refs_6_), slice={[0:464], [0:512]} | slice | bytes 950272 | tf_op jit(solution)/shard_map/slice | solution.py:31
  82.3 1.9 %collective-permute-start.3 = (bf16[464,512]{1,0:T(8,128)(2,1)}, bf16[464,512]{1,0:T(8,128)(2,1)}, u32[]{:S(2)}, u32[]{:S(2)}) collective-permute-start(bf16[464,512]{1,0:T(8,128)(2,1)} %slice.8), channel_id=1, source_target_pairs={{0,1},{1,0},{2,3},{3,2},{4,5},{5,4},{6,7},{7,6},{8,9},{9,8},{10,11... | collective-permute-start | bytes 1425416 | tf_op jit(solution)/shard_map/ppermute | solution.py:31
  84.2 0.0 collective-permute-done.6.refs_5_
  84.2 1.8 %slice.9 = bf16[384,512]{1,0:T(8,128)(2,1)} slice(bf16[848,512]{1,0:T(8,128)(2,1)} %collective-permute-done.6.refs_5_), slice={[464:848], [0:512]} | slice | bytes 786432 | tf_op jit(solution)/shard_map/slice | solution.py:32
  86.0 2.6 %collective-permute-start.7 = (bf16[384,512]{1,0:T(8,128)(2,1)}, bf16[384,512]{1,0:T(8,128)(2,1)S(1)}, u32[]{:S(2)}, u32[]{:S(2)}) collective-permute-start(bf16[384,512]{1,0:T(8,128)(2,1)} %slice.9), channel_id=1, source_target_pairs={{0,7},{1,2},{2,1},{3,4},{4,3},{5,6},{6,5},{7,0},{8,15},{9,10},{10,... | collective-permute-start | bytes 1179656 | tf_op jit(solution)/shard_map/ppermute | solution.py:32
  88.6 0.1 copy.22.ids_ref
  88.7 0.0 all-to-all-done.1
  88.8 4.8 %all-gather = bf16[64,24,256]{2,1,0:T(8,128)(2,1)S(1)} all-gather(bf16[32,24,256]{2,1,0:T(8,128)(2,1)} %all-to-all-done.1), channel_id=2, replica_groups=mesh['vocab_0'=8,'vocab_1'=4,'vocab_2'=2,'grp'=8] {'vocab_2'}, dimensions={0}, use_global_device_ids=true | all-gather | bytes 1179648 | tf_op jit(solution)/shard_map/all_gather | solution.py:318
  93.6 0.0 copy-done.2
  93.6 0.0 copy-start.4
  93.6 1.2 copy-done.4
  94.8 4.1 %shard_map.124 = (bf16[256,1536]{1,0:T(8,128)(2,1)S(1)}, f32[256,512]{1,0:T(8,128)S(1)}, f32[256,1024]{1,0:T(8,128)S(1)}, bf16[2,256,512]{2,1,0:T(8,128)(2,1)S(1)}, bf16[2,64,512]{2,1,0:T(8,128)(2,1)S(1)}) custom-call(s32[8]{0:T(128)S(1)} %and_select_fusion.1.owner_ref, bf16[1536,256]{1,0:T(8,128)(2,1)S(1)} %bitcast.21, bf16[256,4096]{1,0:T(8,128)(2,1)S(1)} %copy-done.1, ...), custom_call_target="tpu_custom_call" | custom-call | flops 1778384896 | bytes 1048576 | tf_op jit(solution)/shard_map/pallas_call | solution.py:53
  98.8 0.0 collective-permute-done.7.second_ref
  98.9 0.0 collective-permute-done.3.first_ref
  98.9 3.1 %shard_map.125 = f32[8,1,3072]{2,1,0:T(1,128)S(1)} custom-call(s32[8]{0:T(128)S(1)} %and_select_fusion.1.owner_ref, bf16[464,512]{1,0:T(8,128)(2,1)} %collective-permute-done.3.first_ref, bf16[384,512]{1,0:T(8,128)(2,1)S(1)} %collective-permute-done.7.second_ref, bf16[256,4096]{1,0:T(8,128)(2,1)S(1)} %copy-done.1, ...), custom_call_target="tpu_custom_call" | custom-call | flops 222298112 | bytes 1048576 | tf_op jit(solution)/shard_map/pallas_call | solution.py:53
  102.0 0.0 copy-start.6
  102.0 10.7 %all_to_all.20.stats_ref = f32[8,1,3072]{2,1,0:T(1,128)S(1)} all-to-all(f32[8,1,3072]{2,1,0:T(1,128)S(1)} %shard_map.125), channel_id=1, replica_groups=mesh['vocab_0'=8,'vocab_1'=4,'vocab_2'=2,'grp'=8] {'vocab_1','vocab_2'}, dimensions={0} | all-to-all | bytes 196608 | tf_op jit(solution)/shard_map/all_to_all | solution.py:354
  112.7 0.7 shard_map.126
  113.5 6.2 %all-to-all-start.3 = ((f32[8,1,3072]{2,1,0:T(1,128)}), f32[8,1,3072]{2,1,0:T(1,128)S(1)}, u32[]{:S(2)}, u32[]{:S(2)}) async-start(f32[8,1,3072]{2,1,0:T(1,128)} %shard_map.126), calls=%async_computation.3 | async-start | bytes 196608 | tf_op jit(solution)/shard_map/all_to_all | solution.py:358
  119.6 0.0 copy-done
  119.6 0.6 fusion.1.scores_ref
  120.3 7.0 %all-to-all-done.3.stats_ref = f32[8,1,3072]{2,1,0:T(1,128)S(1)} async-done(((f32[8,1,3072]{2,1,0:T(1,128)}), f32[8,1,3072]{2,1,0:T(1,128)S(1)}, u32[]{:S(2)}, u32[]{:S(2)}) %all-to-all-start.3) | async-done | bytes 98336 | tf_op jit(solution)/shard_map/all_to_all | solution.py:358
  127.3 0.0 copy-done.6
  127.3 0.7 shard_map.127
  (4 shorter events, 0.1 us)
Async XLA Ops:
  0.6 119.0 %copy-start = (bf16[4096,3]{0,1:T(4,128)(2,1)S(1)}, bf16[4096,3]{0,1:T(4,128)(2,1)}, u32[]{:S(2)}) copy-start(bf16[4096,3]{0,1:T(4,128)(2,1)} %param.13) | copy-start | bytes 73732
  0.6 66.7 %copy-start.1 = (bf16[256,4096]{1,0:T(8,128)(2,1)S(1)}, bf16[256,4096]{1,0:T(8,128)(2,1)}, u32[]{:S(2)}) copy-start(bf16[256,4096]{1,0:T(8,128)(2,1)} %hidden_ref.5) | copy-start | bytes 6291460
  3.1 30.7 %collective-permute-start = (bf16[848,512]{1,0:T(8,128)(2,1)}, bf16[848,512]{1,0:T(8,128)(2,1)S(1)}, u32[]{:S(2)}, u32[]{:S(2)}) collective-permute-start(bf16[848,512]{1,0:T(8,128)(2,1)} %shard_map.122.refs_0_), channel_id=1, source_target_pairs={{0,7},{1,2},{2,1},{3,4},{4,3},{5,6},{6,5},{7,0},{8,15},{9,10},{10,... | collective-permute-start | bytes 2605064 | tf_op jit(solution)/shard_map/ppermute | solution.py:28
  14.6 22.1 %collective-permute-start.4 = (bf16[848,512]{1,0:T(8,128)(2,1)}, bf16[848,512]{1,0:T(8,128)(2,1)}, u32[]{:S(2)}, u32[]{:S(2)}) collective-permute-start(bf16[848,512]{1,0:T(8,128)(2,1)} %shard_map.122.refs_0_), channel_id=1, source_target_pairs={{0,1},{1,0},{2,3},{3,2},{4,5},{5,4},{6,7},{7,6},{8,9},{9,8},{10,11... | collective-permute-start | bytes 2605064 | tf_op jit(solution)/shard_map/ppermute | solution.py:27
  33.8 33.6 %copy-start.3 = (bf16[848,512]{1,0:T(8,128)(2,1)}, bf16[848,512]{1,0:T(8,128)(2,1)S(1)}, u32[]{:S(2)}) copy-start(bf16[848,512]{1,0:T(8,128)(2,1)S(1)} %collective-permute-done.refs_2_) | copy-start | bytes 2605060
  33.8 23.0 %collective-permute-start.1 = (bf16[848,512]{1,0:T(8,128)(2,1)S(1)}, bf16[848,512]{1,0:T(8,128)(2,1)}, u32[]{:S(2)}, u32[]{:S(2)}) collective-permute-start(bf16[848,512]{1,0:T(8,128)(2,1)S(1)} %collective-permute-done.refs_2_), channel_id=1, source_target_pairs={{0,1},{1,0},{2,3},{3,2},{4,5},{5,4},{6,7},{7,6},{8,9},{9,8},{10,11... | collective-permute-start | bytes 2605064 | tf_op jit(solution)/shard_map/ppermute | solution.py:27
  36.7 23.6 %collective-permute-start.5 = (bf16[848,512]{1,0:T(8,128)(2,1)}, bf16[848,512]{1,0:T(8,128)(2,1)}, u32[]{:S(2)}, u32[]{:S(2)}) collective-permute-start(bf16[848,512]{1,0:T(8,128)(2,1)} %collective-permute-done.4.refs_1_), channel_id=1, source_target_pairs={{0,7},{1,2},{2,1},{3,4},{4,3},{5,6},{6,5},{7,0},{8,15},{9,10},{10,... | collective-permute-start | bytes 2605064 | tf_op jit(solution)/shard_map/ppermute | solution.py:28
  46.4 27.1 %copy-start.5 = (s32[256]{0:T(256)S(1)}, s32[256]{0:T(256)}, u32[]{:S(2)}) copy-start(s32[256]{0:T(256)} %param.20) | copy-start | bytes 3076
  47.1 20.3 %all-to-all-start = ((bf16[32,24,128]{2,1,0:T(8,128)(2,1)}), bf16[32,24,128]{2,1,0:T(8,128)(2,1)S(1)}, u32[]{:S(2)}, u32[]{:S(2)}) async-start(bf16[32,24,128]{2,1,0:T(8,128)(2,1)} %dynamic-slice_bitcast_fusion), calls=%async_computation | async-start | bytes 393216 | tf_op jit(solution)/shard_map/all_to_all | solution.py:311
  56.8 23.6 %collective-permute-start.2 = (bf16[848,512]{1,0:T(8,128)(2,1)}, bf16[848,512]{1,0:T(8,128)(2,1)}, u32[]{:S(2)}, u32[]{:S(2)}) collective-permute-start(bf16[848,512]{1,0:T(8,128)(2,1)} %collective-permute-done.1.refs_3_), channel_id=1, source_target_pairs={{0,7},{1,2},{2,1},{3,4},{4,3},{5,6},{6,5},{7,0},{8,15},{9,10},{10,... | collective-permute-start | bytes 2605064 | tf_op jit(solution)/shard_map/ppermute | solution.py:28
  60.3 23.9 %collective-permute-start.6 = (bf16[848,512]{1,0:T(8,128)(2,1)}, bf16[848,512]{1,0:T(8,128)(2,1)}, u32[]{:S(2)}, u32[]{:S(2)}) collective-permute-start(bf16[848,512]{1,0:T(8,128)(2,1)} %collective-permute-done.5.refs_4_), channel_id=1, source_target_pairs={{0,1},{1,0},{2,3},{3,2},{4,5},{5,4},{6,7},{7,6},{8,9},{9,8},{10,11... | collective-permute-start | bytes 2605064 | tf_op jit(solution)/shard_map/ppermute | solution.py:27
  68.1 25.5 %copy-start.2 = (bf16[848,512]{1,0:T(8,128)(2,1)S(1)}, bf16[848,512]{1,0:T(8,128)(2,1)}, u32[]{:S(2)}) copy-start(bf16[848,512]{1,0:T(8,128)(2,1)} %shard_map.122.refs_0_) | copy-start | bytes 2605060
  68.9 19.8 %all-to-all-start.1 = ((bf16[32,24,256]{2,1,0:T(8,128)(2,1)}), bf16[32,24,256]{2,1,0:T(8,128)(2,1)}, u32[]{:S(2)}, u32[]{:S(2)}) async-start(bf16[32,24,256]{2,1,0:T(8,128)(2,1)} %broadcast_in_dim.10), calls=%async_computation.1 | async-start | bytes 786432 | tf_op jit(solution)/shard_map/all_to_all | solution.py:41
  82.3 16.6 %collective-permute-start.3 = (bf16[464,512]{1,0:T(8,128)(2,1)}, bf16[464,512]{1,0:T(8,128)(2,1)}, u32[]{:S(2)}, u32[]{:S(2)}) collective-permute-start(bf16[464,512]{1,0:T(8,128)(2,1)} %slice.8), channel_id=1, source_target_pairs={{0,1},{1,0},{2,3},{3,2},{4,5},{5,4},{6,7},{7,6},{8,9},{9,8},{10,11... | collective-permute-start | bytes 1425416 | tf_op jit(solution)/shard_map/ppermute | solution.py:31
  86.0 12.9 %collective-permute-start.7 = (bf16[384,512]{1,0:T(8,128)(2,1)}, bf16[384,512]{1,0:T(8,128)(2,1)S(1)}, u32[]{:S(2)}, u32[]{:S(2)}) collective-permute-start(bf16[384,512]{1,0:T(8,128)(2,1)} %slice.9), channel_id=1, source_target_pairs={{0,7},{1,2},{2,1},{3,4},{4,3},{5,6},{6,5},{7,0},{8,15},{9,10},{10,... | collective-permute-start | bytes 1179656 | tf_op jit(solution)/shard_map/ppermute | solution.py:32
  93.6 1.2 copy-start.4
  102.0 25.3 %copy-start.6 = (s32[256,3]{0,1:T(4,128)S(1)}, s32[256,3]{0,1:T(4,128)}, u32[]{:S(2)}) copy-start(s32[256,3]{0,1:T(4,128)} %param.21) | copy-start | bytes 9220
  113.5 13.9 %all-to-all-start.3 = ((f32[8,1,3072]{2,1,0:T(1,128)}), f32[8,1,3072]{2,1,0:T(1,128)S(1)}, u32[]{:S(2)}, u32[]{:S(2)}) async-start(f32[8,1,3072]{2,1,0:T(1,128)} %shard_map.126), calls=%async_computation.3 | async-start | bytes 196608 | tf_op jit(solution)/shard_map/all_to_all | solution.py:358
